TPU v7x, 512 devices: a 4x2x32 block of a 4x8x32 slice. The times are simulated.
512 devices in a mesh: grp: 2 (over y), blk: 128 (over z, x), uly: 2 (over core).
Axes of the slice: x: 4, y: 2, z: 32, core: 2. Of those that a mesh axis runs over, the one named last changes fastest.
The devices are a block of a 4x8x32 slice.
Arguments:
- query: bfloat16 [8192, 1152], P(('grp', 'blk', 'uly')), parts along dimension 0, may hold values from -6 to 6
- key: bfloat16 [8192, 1152], P(('grp', 'blk', 'uly')), parts along dimension 0, may hold values from -6 to 6
- value: bfloat16 [8192, 1152], P(('grp', 'blk', 'uly')), parts along dimension 0, may hold values from -6 to 6
- q_gain: float32 [96], replicated, may hold values from 1 to 2.5
- k_gain: float32 [96], replicated, may hold values from 1 to 2.5
- out_weight: bfloat16 [1152, 2304], P('uly'), may hold values from -0.1875 to 0.1875
Outputs:
- mixed: bfloat16 [8192, 2304], P(('grp', 'blk', 'uly')), parts along dimension 0
There are 2 independent parts, one for each index of `grp`. A program takes and returns all parts, laid end to end along the dimension named above; an argument that names none is the same for every part. Nothing has to cross between parts.
All inputs are finite; a program needn't handle non-finite values.
Results may differ from a plain program's by a relative error of at most 0.012.
Values may be sent and summed in bfloat16 or wider, within the bound.
A program may use at most 128 MiB of HBM per device.

v0:
```python
import jax
import jax.numpy as jnp
from jax import lax
from jax.sharding import Mesh
from jax.sharding import PartitionSpec as P

H = 12
HD = 96
GRP_BLK_ULY = ("grp", "blk_0", "blk_1", "uly")


def whole_of(shard, axes, dim):
    if not axes:
        return shard
    nearer = lax.all_gather(shard, axes[-1], axis=dim, tiled=True)
    return whole_of(nearer, axes[:-1], dim)


def split_up(shard, dim, length):
    dims = shard.shape
    blocks = shard.reshape(*dims[:dim], length, dims[dim] // length, *dims[dim + 1 :])
    return jnp.moveaxis(blocks, dim, 0)


def sent_and_summed(shard, axis, dim):
    length = lax.axis_size(axis)
    blocks = lax.all_to_all(split_up(shard, dim, length), axis, 0, 0, tiled=True)
    return jnp.sum(blocks.astype(jnp.float32), axis=0)


def normed(data, gain):
    tok_rows = data.shape[0]
    grid = data.astype(jnp.float32).reshape(tok_rows, H, HD)
    meansq = jnp.mean(grid * grid, axis=-1, keepdims=True)
    return (grid * lax.rsqrt(meansq + 1e-06) * gain).astype(jnp.bfloat16).reshape(tok_rows, H * HD)


def attend_block(query_heads, kv_piece):
    length = kv_piece.shape[1]
    head_count = query_heads.shape[1]
    key_heads = kv_piece[0].reshape(length, head_count, HD)
    value_heads = kv_piece[1].reshape(length, head_count, HD)
    score_scale = float(HD) ** (-0.5)
    scores = (
        jnp.einsum("qhd,khd->hqk", query_heads, key_heads, preferred_element_type=jnp.float32)
        * score_scale
    )
    expd = jnp.exp(scores)
    total_weight = jnp.sum(expd, axis=-1).T
    weighted = jnp.einsum(
        "hqk,khd->qhd", expd.astype(jnp.bfloat16), value_heads, preferred_element_type=jnp.float32
    )
    return (weighted, total_weight)


def on_device(query, key, value, q_gain, k_gain, out_weight):
    query_normed = normed(query, q_gain)
    key_normed = normed(key, k_gain)
    query_group, key_group, value_group = (
        lax.all_to_all(query_normed, "uly", split_axis=1, concat_axis=0, tiled=True),
        lax.all_to_all(key_normed, "uly", split_axis=1, concat_axis=0, tiled=True),
        lax.all_to_all(value, "uly", split_axis=1, concat_axis=0, tiled=True),
    )
    row_count = query_group.shape[0]
    local_heads = query_group.shape[1] // HD
    query_heads = query_group.reshape(row_count, local_heads, HD)
    kv_stack = jnp.stack([key_group, value_group])
    weighted, total_weight = attend_block(query_heads, whole_of(kv_stack, ("blk_1", "blk_0"), 1))
    attn = (
        (weighted / total_weight[:, :, None])
        .astype(jnp.bfloat16)
        .reshape(row_count, local_heads * HD)
    )
    mixed = sent_and_summed(
        jnp.dot(attn, out_weight, preferred_element_type=jnp.float32).astype(jnp.bfloat16), "uly", 0
    )
    return mixed.astype(jnp.bfloat16)


def solution(mesh):
    split = Mesh(
        mesh.devices.reshape(mesh.shape["grp"], 32, 4, mesh.shape["uly"]),
        ("grp", "blk_0", "blk_1", "uly"),
    )
    in_specs = (
        P(GRP_BLK_ULY, None),
        P(GRP_BLK_ULY, None),
        P(GRP_BLK_ULY, None),
        P(),
        P(),
        P("uly", None),
    )
    out_specs = P(GRP_BLK_ULY, None)
    return jax.shard_map(
        on_device, mesh=split, in_specs=in_specs, out_specs=out_specs, check_vma=False
    )
```

profile of v0, /device:TPU:33, one launch (start us, length us, event | category | flops | bytes accessed | tf_op | source)
XLA Modules:
  0.0 334.8 jit_solution(16086594618422082272)
XLA Ops:
  6.6 0.9 convert_multiply_fusion.3
  7.5 0.1 mul.67
  7.6 0.1 reduce_sum.39
  7.8 0.1 mul.69
  7.9 0.7 mul.71
  8.7 0.8 fusion.13
  9.5 0.1 all_to_all.39
  9.6 0.6 copy.22
  10.2 44.7 %all-to-all-start = ((bf16[16,2,576]{2,0,1:T(8,128)(2,1)}), bf16[16,2,576]{2,0,1:T(8,128)(2,1)S(1)}, u32[]{:S(2)}, u32[]{:S(2)}) async-start(bf16[16,2,576]{2,0,1:T(8,128)(2,1)} %copy.22), calls=%async_computation | async-start | bytes 81920 | tf_op jit(solution)/shard_map/all_to_all | solution.py:61
  54.9 0.9 all_to_all.42
  55.8 0.2 all-to-all-done
  56.0 3.8 %all_to_all.53 = bf16[16,2,576]{2,0,1:T(8,128)(2,1)S(1)} all-to-all(bf16[16,2,576]{2,0,1:T(8,128)(2,1)S(1)} %copy.23), channel_id=1, replica_groups=mesh['grp'=2,'blk_0'=32,'blk_1'=4,'uly'=2] {'uly'}, dimensions={1} | all-to-all | bytes 73728 | tf_op jit(solution)/shard_map/all_to_all | solution.py:62
  59.7 0.6 pad_maximum_fusion
  60.5 101.1 %all-gather.3.cloned.1.call-done = bf16[2,1024,576]{2,1,0:T(8,128)(2,1)} async-done(((bf16[2,32,576]{2,1,0:T(8,128)(2,1)}), bf16[2,1024,576]{2,1,0:T(8,128)(2,1)}) %all-gather.3.cloned.1.call-update) | async-done | bytes 2359312 | tf_op jit(solution)/shard_map/all_gather | solution.py:15
  161.7 0.8 convert_multiply_fusion.1
  162.5 0.1 mul.76
  162.6 0.1 reduce_sum.40
  162.8 0.1 mul.78
  163.0 0.1 all_to_all.45
  163.1 25.3 %all_to_all.54 = bf16[16,2,576]{2,0,1:T(8,128)(2,1)S(1)} all-to-all(bf16[16,2,576]{2,0,1:T(8,128)(2,1)S(1)} %copy.25), channel_id=1, replica_groups=mesh['grp'=2,'blk_0'=32,'blk_1'=4,'uly'=2] {'uly'}, dimensions={1} | all-to-all | bytes 73728 | tf_op jit(solution)/shard_map/all_to_all | solution.py:60
  188.5 0.1 reshape.50
  188.6 104.1 %all-gather.5.cloned.1.call-done = bf16[2,4096,576]{2,1,0:T(8,128)(2,1)} async-done(((bf16[2,1024,576]{2,1,0:T(8,128)(2,1)}), bf16[2,4096,576]{2,1,0:T(8,128)(2,1)}) %all-gather.5.cloned.1.call-update) | async-done | bytes 9437200 | tf_op jit(solution)/shard_map/all_gather | solution.py:15
  292.6 8.9 %fusion.17 = (bf16[1,4096,576]{2,1,0:T(8,128)(2,1)}, bf16[1,4096,576]{2,1,0:T(8,128)(2,1)}) fusion(bf16[2,4096,576]{2,1,0:T(8,128)(2,1)} %all-gather.5.cloned.1.call-done), kind=kLoop, calls=%fused_computation.20 | loop fusion | bytes 18874368 | tf_op jit(solution)/shard_map/slice | solution.py:41
  301.5 7.6 %copy.26 = bf16[1,4096,576]{1,2,0:T(8,128)(2,1)} copy(bf16[1,4096,576]{2,1,0:T(8,128)(2,1)} %get-tuple-element.5) | data formatting | bytes 9437184 | tf_op jit(solution)/shard_map/slice | solution.py:41
  309.2 7.6 %copy.24 = bf16[1,4096,576]{1,2,0:T(8,128)(2,1)} copy(bf16[1,4096,576]{2,1,0:T(8,128)(2,1)} %get-tuple-element.6) | data formatting | bytes 9437184 | tf_op jit(solution)/shard_map/slice | solution.py:42
  316.8 3.5 %fusion.18 = (f32[6,32]{1,0:T(8,128)S(1)}, bf16[6,32,4096]{2,1,0:T(8,128)(2,1)S(1)}) fusion(bf16[4096,6,96]{0,2,1:T(8,128)(2,1)} %bitcast.22, bf16[32,6,96]{2,1,0:T(8,128)(2,1)S(1)} %reshape.50), kind=kOutput, calls=%fused_computation.21 | convolution fusion | flops 153354048 | bytes 6329088 | tf_op jit(solution)/shard_map/qhd,khd->hqk/dot_general | solution.py:45
  320.3 0.3 copy-done.1
  320.5 1.8 fusion.9
  322.4 0.1 reshape.51
  322.5 0.5 convolution_convert_fusion
  323.0 4.3 %all_to_all.55 = bf16[2,16,2304]{2,1,0:T(8,128)(2,1)S(1)} all-to-all(bf16[2,16,2304]{2,1,0:T(8,128)(2,1)S(1)} %bitcast.24), channel_id=1, replica_groups=mesh['grp'=2,'blk_0'=32,'blk_1'=4,'uly'=2] {'uly'}, dimensions={0} | all-to-all | bytes 294912 | tf_op jit(solution)/shard_map/all_to_all | solution.py:27
  327.3 0.7 reduce_sum.42
  (22 shorter events, 0.6 us)
Async XLA Ops:
  6.5 315.9 %copy-start = (bf16[576,2304]{1,0:T(8,128)(2,1)S(1)}, bf16[576,2304]{1,0:T(8,128)(2,1)}, u32[]{:S(2)}) copy-start(bf16[576,2304]{1,0:T(8,128)(2,1)} %param.11) | copy-start | bytes 7962628
  6.6 156.4 %copy-start.2 = (bf16[16,1152]{1,0:T(8,128)(2,1)S(1)}, bf16[16,1152]{1,0:T(8,128)(2,1)}, u32[]{:S(2)}) copy-start(bf16[16,1152]{1,0:T(8,128)(2,1)} %param.6) | copy-start | bytes 110596
  6.6 156.3 %copy-start.3 = (f32[96]{0:T(128)S(1)}, f32[96]{0:T(128)}, u32[]{:S(2)}) copy-start(f32[96]{0:T(128)} %param.9) | copy-start | bytes 1156
  10.2 45.8 %all-to-all-start = ((bf16[16,2,576]{2,0,1:T(8,128)(2,1)}), bf16[16,2,576]{2,0,1:T(8,128)(2,1)S(1)}, u32[]{:S(2)}, u32[]{:S(2)}) async-start(bf16[16,2,576]{2,0,1:T(8,128)(2,1)} %copy.22), calls=%async_computation | async-start | bytes 81920 | tf_op jit(solution)/shard_map/all_to_all | solution.py:61
  54.9 106.7 %all-gather.3.cloned.1.call-start = ((), (), s32[]{:S(2)}) async-start(), calls=%async_computation.4 | async-start | bytes 2703360 | tf_op jit(solution)/shard_map/all_gather | solution.py:15
  60.4 232.2 %all-gather.5.cloned.1.call-start = ((), (), s32[]{:S(2)}) async-start(), calls=%async_computation.5 | async-start | bytes 13107200 | tf_op jit(solution)/shard_map/all_gather | solution.py:15
  316.8 3.8 %copy-start.1 = (bf16[1,4096,576]{1,2,0:T(8,128)(2,1)S(1)}, bf16[1,4096,576]{1,2,0:T(8,128)(2,1)}, u32[]{:S(2)}) copy-start(bf16[1,4096,576]{1,2,0:T(8,128)(2,1)} %copy.24) | copy-start | bytes 14155780
Sparse Core Ops, SparseCore 0:
  60.5 101.0 all-gather.2
  163.7 128.8 all-gather.4
where the time goes:
time: 336 us; the launch traced here: 335 us
  waiting for transfers between devices  205 us (61%)
  starting transfers between devices  44.8 us (13%)
  blocking collectives  33.4 us (10%)
  local copies, waits for them, and re-layouts  27.8 us (8%)
  between operations  13.6 us (4%)
  matrix products  5.82 us (2%)
  other arithmetic  4.04 us (1%)
    all_gather x2, waiting for transfers between devices, whole_of(): nearer = lax.all_gather(shard, axes[-1], axis=dim, tiled=True)  205 us
    all_to_all x1, starting transfers between devices, on_device(): lax.all_to_all(key_normed, 'uly', split_axis=1, concat_axis=0, tiled=True)  44.7 us
    all_to_all x1, blocking collectives, on_device(): lax.all_to_all(query_normed, 'uly', split_axis=1, concat_axis=0, tiled=True)  25.3 us
    slice x2, local copies, waits for them, and re-layouts, attend_block(): key_heads = kv_piece[0].reshape(length, head_count, HD)  16.5 us
    slice x1, local copies, waits for them, and re-layouts, attend_block(): value_heads = kv_piece[1].reshape(length, head_count, HD)  7.59 us
  transfers between devices with their start and end apart: 3, of which 3 were waited for; matrix products, arithmetic and copies ran while one was open for 0% of the time, Pallas kernels for 0%

commit v1 on v0

v1 whole, which is shorter than its diff:
```python
import functools
import math

import jax
import jax.numpy as jnp
from jax import lax
from jax.experimental import pallas as pl
from jax.experimental.pallas import tpu as pltpu
from jax.sharding import PartitionSpec as P

HD = 96
PAD = 128
COLUMNS = 4
ROWS = 2
RING_CORE = 1
MESH = pl.DeviceIdType.MESH
TN = (((1,), (1,)), ((), ()))


def kernel(
    nodes,
    heads,
    query,
    key,
    value,
    q_gain,
    k_gain,
    weight,
    mixed,
    stage,
    key_raw,
    value_raw,
    query_raw,
    turned,
    gain_pad,
    own,
    opposite,
    ring,
    q_heads,
    totals,
    parts_out,
    parts_in,
    whole_weight,
    stage_sem,
    feed_send,
    feed_recv,
    ring_send,
    ring_recv,
    far_send,
    far_recv,
    back_send,
    back_recv,
    weight_sem,
):
    f32, bf16 = jnp.float32, jnp.bfloat16
    block = lax.axis_index("blk")
    core = lax.axis_index("uly")
    z, x = lax.div(block, COLUMNS), lax.rem(block, COLUMNS)
    z_block, z_row = lax.div(z, ROWS), lax.rem(z, ROWS)
    on_ring = core == RING_CORE
    tokens = query.shape[0]
    window = 3 * PAD
    lanes = 2 * PAD
    group = heads * HD
    line = 2 * COLUMNS * tokens
    half = nodes // 2
    pieces = 2 * heads

    def device(row, column, a_core):
        return {"blk": row * COLUMNS + column, "uly": a_core}

    def other_row(r):
        return z_block * ROWS + lax.rem(z_row + r, ROWS)

    def other_column(d):
        return lax.rem(x + d, COLUMNS)

    ahead = lax.rem(z + ROWS, nodes * ROWS)
    behind = lax.rem(z + (nodes - 1) * ROWS, nodes * ROWS)

    staged = [
        pltpu.make_async_copy(src, stage.at[i], stage_sem.at[i])
        for i, src in enumerate((key, value, query))
    ]
    for copy in staged:
        copy.start()

    barrier = pltpu.get_barrier_semaphore()

    def greet(dev):
        pl.semaphore_signal(barrier, inc=1, device_id=dev, device_id_type=MESH)

    for r in range(ROWS):
        for d in range(COLUMNS):
            if (r, d) != (0, 0):
                greet(device(other_row(r), other_column(d), RING_CORE))
    greet(device(z, x, 1 - core))

    @pl.when(on_ring)
    def _():
        for r in range(ROWS):
            for d in range(COLUMNS):
                if (r, d) != (0, 0):
                    greet(device(other_row(r), other_column(d), 1 - RING_CORE))
        greet(device(ahead, x, RING_CORE))
        greet(device(behind, x, RING_CORE))
        pl.semaphore_wait(barrier, 2 * ROWS * COLUMNS - 1 + 2)

    @pl.when(core != RING_CORE)
    def _():
        pl.semaphore_wait(barrier, ROWS * COLUMNS)

    place = pl.ds(pl.multiple_of((x * 2 + core) * tokens, tokens), tokens)

    def feed(i, r, d):
        column = other_column(d)
        dst = (key_raw, value_raw, query_raw.at[z_row])[i].at[place]
        recv = feed_recv.at[i] if i < 2 else feed_recv.at[2 + z_row]
        return pltpu.make_async_remote_copy(
            src_ref=stage.at[i, :, pl.ds(pl.multiple_of(column * lanes, PAD), window)],
            dst_ref=dst,
            send_sem=feed_send.at[i * COLUMNS + d if i < 2 else (2 + r) * COLUMNS + d],
            recv_sem=recv,
            device_id=device(other_row(r), column, RING_CORE),
            device_id_type=MESH,
        )

    def own_feed(i):
        dst = (key_raw, value_raw, query_raw.at[z_row])[i].at[place]
        recv = feed_recv.at[i] if i < 2 else feed_recv.at[2 + z_row]
        src = (key, value, query)[i]
        return pltpu.make_async_copy(
            src.at[:, pl.ds(pl.multiple_of(x * lanes, PAD), window)], dst, recv
        )

    feeds = [(i, r, d) for i in range(3) for r in range(ROWS if i == 2 else 1) for d in (2, 1, 3, 0)]
    for i, r, d in feeds:
        if (r, d) == (0, 2):
            staged[i].wait()
        if (r, d) == (0, 0):

            @pl.when(on_ring)
            def _():
                own_feed(i).start()

            @pl.when(core != RING_CORE)
            def _():
                feed(i, r, d).start()

        else:
            feed(i, r, d).start()

    depth = weight.shape[0]
    mine = whole_weight.at[pl.ds(pl.multiple_of(core * depth, 16), depth)]
    local_weight = pltpu.make_async_copy(weight, mine, weight_sem.at[0])
    sent_weight = pltpu.make_async_remote_copy(
        src_ref=weight,
        dst_ref=mine,
        send_sem=weight_sem.at[1],
        recv_sem=weight_sem.at[2],
        device_id=device(z, x, 1 - core),
        device_id_type=MESH,
    )
    local_weight.start()
    sent_weight.start()

    def give_back(r, d, c):
        column, a_core = other_column(d), lax.rem(core + c, 2)
        row = lax.rem(z_row + r, ROWS)
        start = row * line + (column * 2 + a_core) * tokens
        return pltpu.make_async_remote_copy(
            src_ref=parts_out.at[pl.ds(pl.multiple_of(start, tokens), tokens)],
            dst_ref=parts_in.at[z_row, x],
            send_sem=back_send.at[(r * COLUMNS + d) * 2 + c],
            recv_sem=back_recv.at[z_row * COLUMNS + x],
            device_id=device(other_row(r), column, a_core),
            device_id_type=MESH,
        )

    backs = [(r, d, c) for r in range(ROWS) for d in range(COLUMNS) for c in range(2)]

    @pl.when(on_ring)
    def _():
        for i, gain in enumerate((q_gain, k_gain)):
            gain_pad[...] = jnp.zeros_like(gain_pad)
            gain_pad[:, 0:HD] = jnp.broadcast_to(gain[...], (PAD, HD))
            turned[i, 0:PAD, :] = gain_pad[...].T
        q_column, k_column = turned[0, 0:HD, :], turned[1, 0:HD, :]
        first = x * (group - lanes)

        def head_of(i, h):
            return turned[i, pl.ds(pl.multiple_of(first + h * HD, 32), HD), :]

        def normed(data, gain):
            meansq = jnp.mean(data * data, axis=0, keepdims=True)
            return data * lax.rsqrt(meansq + 1e-06) * gain

        pltpu.make_async_copy(key_raw, key_raw, feed_recv.at[0]).wait()
        turned[0] = key_raw[...].astype(f32).T
        for h in range(heads):
            own[2 * h] = normed(head_of(0, h), k_column).astype(bf16)
        pltpu.make_async_copy(value_raw, value_raw, feed_recv.at[1]).wait()
        turned[1] = value_raw[...].astype(f32).T
        for h in range(heads):
            own[2 * h + 1] = head_of(1, h).astype(bf16)

        def to(way, slot, p, src, step):
            if isinstance(step, int) and step == half - 1:
                dst, send, recv = opposite.at[p], far_send.at[p], far_recv.at[p]
            else:
                dst, send, recv = ring.at[way, step, p], ring_send.at[way, step, p], ring_recv.at[way, step, p]
            return pltpu.make_async_remote_copy(
                src_ref=src,
                dst_ref=dst,
                send_sem=send,
                recv_sem=recv,
                device_id=device(ahead if way == 0 else behind, x, RING_CORE),
                device_id_type=MESH,
            )

        for p in range(pieces):
            for way in range(2):
                to(way, 0, p, own.at[p], 0).start()

        for r in range(ROWS):
            rows = query_raw.at[r]
            pltpu.make_async_copy(rows, rows, feed_recv.at[2 + r]).wait()
            turned[0] = query_raw[r].astype(f32).T
            for h in range(heads):
                data = normed(head_of(0, h), q_column)
                data = jnp.concatenate([data, jnp.zeros((PAD - HD, line), f32)], axis=0)
                q_heads[h, r * line : (r + 1) * line, :] = data.T.astype(bf16)

        scale = float(HD) ** (-0.5) * math.log2(math.e)

        def attend(h, keys, values, fresh=False):
            wide = line * len(keys)
            k = jnp.concatenate(
                [jnp.concatenate(keys, axis=1), jnp.zeros((PAD - HD, wide), bf16)], axis=0
            )
            v = jnp.concatenate(
                [jnp.concatenate(values, axis=1), jnp.ones((PAD - HD, wide), bf16)], axis=0
            )
            scores = jnp.dot(q_heads[h], k, preferred_element_type=f32)
            expd = jnp.exp2(scores * scale).astype(bf16)
            total = lax.dot_general(expd, v, TN, preferred_element_type=f32)
            if fresh:
                totals[h] = total
            else:
                totals[h] += total

        for h in range(heads):
            attend(h, [own[2 * h]], [own[2 * h + 1]], True)

        def ring_step(step, last):
            for h in range(heads):
                for p in (2 * h, 2 * h + 1):
                    for way in range(2):
                        to(way, 0, p, own.at[p], step).wait_recv()
                        if not last:
                            to(way, 0, p, ring.at[way, step, p], step + 1).start()
                        elif (p < pieces // 2) == (way == 0):
                            to(way, 0, p, ring.at[way, step, p], half - 1).start()
                attend(
                    h,
                    [ring[0, step, 2 * h], ring[1, step, 2 * h]],
                    [ring[0, step, 2 * h + 1], ring[1, step, 2 * h + 1]],
                )

        def body(step, carry):
            ring_step(step, False)
            return carry

        lax.fori_loop(0, half - 2, body, 0)
        ring_step(half - 2, True)

        lane = lax.broadcasted_iota(jnp.int32, (ROWS * line, PAD), 1)
        for h in range(heads):
            for p in (2 * h, 2 * h + 1):
                way = 0 if p < pieces // 2 else 1
                to(way, 0, p, own.at[p], half - 1).wait_recv()
            attend(h, [opposite[2 * h]], [opposite[2 * h + 1]])
            total = totals[h]
            high = total.astype(bf16)
            low = (total - high.astype(f32)).astype(bf16)
            parts_out[:, h * PAD : (h + 1) * PAD] = jnp.where(lane >= HD + 16, low, high)

        for r, d, c in backs:
            if (r, d, c) != (0, 0, 0):
                give_back(r, d, c).start()
        own_start = z_row * line + (x * 2 + core) * tokens
        parts_in[z_row, x] = parts_out[pl.ds(pl.multiple_of(own_start, tokens), tokens)]

    local_weight.wait()
    sent_weight.wait()
    attn = []
    for i in range(ROWS * COLUMNS):
        r, d = i // COLUMNS, i % COLUMNS
        itself = (z_row == r) & (x == d) & on_ring

        @pl.when(jnp.logical_not(itself))
        def _():
            pltpu.make_async_copy(parts_in.at[r, d], parts_in.at[r, d], back_recv.at[i]).wait()

    for d in range(COLUMNS):
        for h in range(heads):
            part = sum(
                parts_in[r, d, :, h * PAD : (h + 1) * PAD].astype(f32) for r in range(ROWS)
            )
            total_weight = part[:, HD : HD + 1] + part[:, HD + 16 : HD + 17]
            attn.append((part[:, 0:HD] / total_weight).astype(bf16))
    attn = jnp.concatenate(attn, axis=1)
    mixed[...] = jnp.dot(attn, whole_weight[...], preferred_element_type=f32).astype(bf16)

    for i, r, d in feeds:
        if (r, d) == (0, 0):

            @pl.when(core != RING_CORE)
            def _():
                feed(i, r, d).wait_send()

        else:
            feed(i, r, d).wait_send()

    @pl.when(on_ring)
    def _():
        def sent(step, carry):
            for way in range(2):
                for p in range(pieces):
                    pltpu.make_async_copy(
                        ring.at[way, step, p], ring.at[way, step, p], ring_send.at[way, step, p]
                    ).wait()
            return carry

        lax.fori_loop(0, half - 1, sent, 0)
        for p in range(pieces):
            pltpu.make_async_copy(opposite.at[p], opposite.at[p], far_send.at[p]).wait()
        for r, d, c in backs:
            if (r, d, c) != (0, 0, 0):
                give_back(r, d, c).wait_send()


def on_device(lines, query, key, value, q_gain, k_gain, out_weight):
    tokens, width = query.shape
    heads = width // HD // COLUMNS
    nodes = lines // ROWS
    half = nodes // 2
    pieces = 2 * heads
    line = 2 * COLUMNS * tokens
    window = 3 * PAD
    f32, bf16 = jnp.float32, jnp.bfloat16
    hbm = pl.BlockSpec(memory_space=pl.ANY)
    vmem = pl.BlockSpec(memory_space=pltpu.VMEM)
    dma = pltpu.SemaphoreType.DMA
    return pl.pallas_call(
        functools.partial(kernel, nodes, heads),
        out_shape=jax.ShapeDtypeStruct((tokens, out_weight.shape[1]), bf16),
        in_specs=[hbm, hbm, hbm, vmem, vmem, hbm],
        out_specs=vmem,
        scratch_shapes=[
            pltpu.VMEM((3, tokens, width), bf16),
            pltpu.VMEM((line, window), bf16),
            pltpu.VMEM((line, window), bf16),
            pltpu.VMEM((ROWS, line, window), bf16),
            pltpu.VMEM((2, window, line), f32),
            pltpu.VMEM((PAD, PAD), f32),
            pltpu.VMEM((pieces, HD, line), bf16),
            pltpu.VMEM((pieces, HD, line), bf16),
            pltpu.VMEM((2, half - 1, pieces, HD, line), bf16),
            pltpu.VMEM((heads, ROWS * line, PAD), bf16),
            pltpu.VMEM((heads, ROWS * line, PAD), f32),
            pltpu.VMEM((ROWS * line, heads * PAD), bf16),
            pltpu.VMEM((ROWS, COLUMNS, tokens, heads * PAD), bf16),
            pltpu.VMEM((2 * out_weight.shape[0], out_weight.shape[1]), bf16),
            dma((3,)),
            dma(((2 + ROWS) * COLUMNS,)),
            dma((2 + ROWS,)),
            dma((2, half - 1, pieces)),
            dma((2, half - 1, pieces)),
            dma((pieces,)),
            dma((pieces,)),
            dma((ROWS * COLUMNS * 2,)),
            dma((ROWS * COLUMNS,)),
            dma((3,)),
        ],
        compiler_params=pltpu.CompilerParams(collective_id=0, has_side_effects=True),
        name="attention",
    )(query, key, value, q_gain.reshape(1, HD), k_gain.reshape(1, HD), out_weight)


def solution(mesh):
    tokens = P(("grp", "blk", "uly"), None)
    return jax.shard_map(
        functools.partial(on_device, mesh.shape["blk"] // COLUMNS),
        mesh=mesh,
        in_specs=(tokens, tokens, tokens, P(), P(), P("uly", None)),
        out_specs=tokens,
        check_vma=False,
    )
```

time: 336 us -> 92.3 us (0.27)
  waiting for transfers between devices: 205 us -> 0 us
  Pallas kernels: 0 us -> 90.5 us
  starting transfers between devices: 44.8 us -> 0 us
  blocking collectives: 33.4 us -> 0 us
  local copies, waits for them, and re-layouts: 27.8 us -> 1.52 us
  between operations: 13.6 us -> 0.01 us
  matrix products: 5.82 us -> 0 us
  other arithmetic: 4.04 us -> 0 us
    all_gather x2 -> x0, waiting for transfers between devices: 205 us -> none  [whole_of(): nearer = lax.all_gather(shard, axes[-1], axis=dim, tiled=True)]
    pallas_call x0 -> x1, Pallas kernels: none -> 90.5 us  [on_device(): pl.pallas_call(functools.partial(kernel, nodes, heads), out_shape=jax.Sha...]
    all_to_all x1 -> x0, starting transfers between devices: 44.7 us -> none  [on_device(): lax.all_to_all(key_normed, 'uly', split_axis=1, concat_axis=0, tiled=True)]
    all_to_all x3 -> x0, blocking collectives: 33.4 us -> none  [the longest x1 25.3 us: on_device(): lax.all_to_all(query_normed, 'uly', split_axis=1, concat_axis=0, tiled=True)]
    slice x3 -> x0, local copies, waits for them, and re-layouts: 24.1 us -> none  [the longest x2 16.5 us: attend_block(): key_heads = kv_piece[0].reshape(length, head_count, HD)]
    dot_general x3 -> x0, matrix products: 5.82 us -> none  [the longest x1 3.49 us: attend_block(): jnp.einsum('qhd,khd->hqk', query_heads, key_heads, preferred_element_type...]
  transfers between devices with their start and end apart: 3 -> 0, of which waited for: 3 -> 0; matrix products, arithmetic and copies ran while one was open for 0% -> 0% of each run, Pallas kernels for 0% -> 0%
where the time goes in v1:
time: 92.3 us; the launch traced here: 92.1 us
  Pallas kernels  90.5 us (98%)
  local copies, waits for them, and re-layouts  1.52 us (2%)
    pallas_call x1, Pallas kernels, on_device(): pl.pallas_call(functools.partial(kernel, nodes, heads), out_shape=jax.Sha...  90.5 us

profile of v1, /device:TPU:33, one launch (start us, length us, event | category | flops | bytes accessed | tf_op | source)
XLA Modules:
  0.0 92.1 jit_solution(12921598640498939943)
XLA Ops:
  0.0 90.5 %attention.1 = bf16[16,2304]{1,0:T(8,128)(2,1)} custom-call(bf16[16,1152]{1,0:T(8,128)(2,1)} %query.1, bf16[16,1152]{1,0:T(8,128)(2,1)} %key.1, bf16[16,1152]{1,0:T(8,128)(2,1)} %value.1, f32[1,96]{1,0:T(1,128)} %bitcast.2, f32[1,96]{1,0:T(1,128)} %bitcast.3, bf16[576,2304]{1,0:T(8,128)(2,1)} %weight.1), custom_call_target="tpu_custom_call" | custom-call | tf_op jit(solution)/shard_map/attention/pallas_call | solution.py:355
  90.6 1.5 %copy.8 = bf16[16,2304]{1,0:T(8,128)(2,1)} copy(bf16[16,2304]{1,0:T(8,128)(2,1)} %attention.1) | data formatting | bytes 147456

commit v2 on v1

--- a/solution.py
+++ b/solution.py
@@ -13,6 +13,7 @@
 COLUMNS = 4
 ROWS = 2
 RING_CORE = 1
+AHEAD = 6
 MESH = pl.DeviceIdType.MESH
 TN = (((1,), (1,)), ((), ()))
 
@@ -34,7 +35,6 @@
     turned,
     gain_pad,
     own,
-    opposite,
     ring,
     q_heads,
     totals,
@@ -46,11 +46,10 @@
     feed_recv,
     ring_send,
     ring_recv,
-    far_send,
-    far_recv,
     back_send,
     back_recv,
     weight_sem,
+    ready,
 ):
     f32, bf16 = jnp.float32, jnp.bfloat16
     block = lax.axis_index("blk")
@@ -63,8 +62,8 @@
     lanes = 2 * PAD
     group = heads * HD
     line = 2 * COLUMNS * tokens
-    half = nodes // 2
     pieces = 2 * heads
+    most = (AHEAD, nodes - 1 - AHEAD)
 
     def device(row, column, a_core):
         return {"blk": row * COLUMNS + column, "uly": a_core}
@@ -75,8 +74,10 @@
     def other_column(d):
         return lax.rem(x + d, COLUMNS)
 
+    node, last_node = z_block, nodes - 1
     ahead = lax.rem(z + ROWS, nodes * ROWS)
-    behind = lax.rem(z + (nodes - 1) * ROWS, nodes * ROWS)
+    behind = lax.rem(z + last_node * ROWS, nodes * ROWS)
+    is_first, is_last = node == 0, node == last_node
 
     staged = [
         pltpu.make_async_copy(src, stage.at[i], stage_sem.at[i])
@@ -102,9 +103,29 @@
             for d in range(COLUMNS):
                 if (r, d) != (0, 0):
                     greet(device(other_row(r), other_column(d), 1 - RING_CORE))
-        greet(device(ahead, x, RING_CORE))
-        greet(device(behind, x, RING_CORE))
-        pl.semaphore_wait(barrier, 2 * ROWS * COLUMNS - 1 + 2)
+
+        @pl.when(jnp.logical_not(is_last))
+        def _():
+            greet(device(ahead, x, RING_CORE))
+
+        @pl.when(is_first)
+        def _():
+            greet(device(behind, x, RING_CORE))
+
+        lower = jnp.where(is_first, 0, 1) + jnp.where(is_last, 1, 0)
+        pl.semaphore_wait(barrier, 2 * ROWS * COLUMNS - 1 + lower)
+
+        @pl.when(jnp.logical_not(is_first))
+        def _():
+            pl.semaphore_signal(
+                ready.at[0], inc=1, device_id=device(behind, x, RING_CORE), device_id_type=MESH
+            )
+
+        @pl.when(is_last)
+        def _():
+            pl.semaphore_signal(
+                ready.at[1], inc=1, device_id=device(ahead, x, RING_CORE), device_id_type=MESH
+            )
 
     @pl.when(core != RING_CORE)
     def _():
@@ -204,23 +225,29 @@
         for h in range(heads):
             own[2 * h + 1] = head_of(1, h).astype(bf16)
 
-        def to(way, slot, p, src, step):
-            if isinstance(step, int) and step == half - 1:
-                dst, send, recv = opposite.at[p], far_send.at[p], far_recv.at[p]
-            else:
-                dst, send, recv = ring.at[way, step, p], ring_send.at[way, step, p], ring_recv.at[way, step, p]
+        def landing(way, step, p, src):
             return pltpu.make_async_remote_copy(
                 src_ref=src,
-                dst_ref=dst,
-                send_sem=send,
-                recv_sem=recv,
-                device_id=device(ahead if way == 0 else behind, x, RING_CORE),
+                dst_ref=ring.at[way, step, p],
+                send_sem=ring_send.at[way, step, p],
+                recv_sem=ring_recv.at[way, step, p],
+                device_id=device(jnp.where(way == 0, ahead, behind), x, RING_CORE),
                 device_id_type=MESH,
             )
 
-        for p in range(pieces):
-            for way in range(2):
-                to(way, 0, p, own.at[p], 0).start()
+        def send_own(way):
+            for p in range(pieces):
+                landing(way, 0, p, own.at[p]).start()
+
+        @pl.when(jnp.logical_not(is_last))
+        def _():
+            pl.semaphore_wait(ready.at[0], 1)
+
+        send_own(0)
+
+        @pl.when(jnp.logical_not(is_first))
+        def _():
+            send_own(1)
 
         for r in range(ROWS):
             rows = query_raw.at[r]
@@ -252,34 +279,57 @@
         for h in range(heads):
             attend(h, [own[2 * h]], [own[2 * h + 1]], True)
 
-        def ring_step(step, last):
+        def opens(m):
+            return jnp.minimum(40 * m, 160 + 20 * m)
+
+        def from_behind(step):
+            m = node - 1 - step
+            return jnp.where(
+                m >= 0, opens(node) + 15 * step, opens(m + nodes) + 50 + 26 * (step + 1)
+            )
+
+        def from_ahead(step):
+            m = node + 1 + step
+            return jnp.where(
+                m < nodes,
+                opens(m) + 50 + 26 * (step + 1),
+                opens(last_node) + 80 + 26 * (last_node - node) + 16 * (m - nodes + 1),
+            )
+
+        def chunk(t, steps):
+            up, down = steps
+            take_up = (down >= most[1]) | ((up < most[0]) & (from_behind(up) <= from_ahead(down)))
+
+            @pl.when(is_first & take_up & (up == 0))
+            def _():
+                pl.semaphore_wait(ready.at[1], 1)
+                send_own(1)
+
+                def held(step, carry):
+                    for p in range(pieces):
+                        landing(1, step + 1, p, ring.at[1, step, p]).start()
+                    return carry
+
+                lax.fori_loop(0, jnp.minimum(down, most[1] - 1), held, 0)
+
+            way = jnp.where(take_up, 0, 1)
+            step = jnp.where(take_up, up, down)
+            passes = jnp.where(take_up, up < most[0] - 1, (down < most[1] - 1) & ~(is_first & (up == 0)))
             for h in range(heads):
                 for p in (2 * h, 2 * h + 1):
-                    for way in range(2):
-                        to(way, 0, p, own.at[p], step).wait_recv()
-                        if not last:
-                            to(way, 0, p, ring.at[way, step, p], step + 1).start()
-                        elif (p < pieces // 2) == (way == 0):
-                            to(way, 0, p, ring.at[way, step, p], half - 1).start()
-                attend(
-                    h,
-                    [ring[0, step, 2 * h], ring[1, step, 2 * h]],
-                    [ring[0, step, 2 * h + 1], ring[1, step, 2 * h + 1]],
-                )
-
-        def body(step, carry):
-            ring_step(step, False)
-            return carry
-
-        lax.fori_loop(0, half - 2, body, 0)
-        ring_step(half - 2, True)
+                    landing(way, step, p, own.at[p]).wait_recv()
+
+                    @pl.when(passes)
+                    def _():
+                        landing(way, step + 1, p, ring.at[way, step, p]).start()
+
+                attend(h, [ring[way, step, 2 * h]], [ring[way, step, 2 * h + 1]])
+            return (jnp.where(take_up, up + 1, up), jnp.where(take_up, down, down + 1))
+
+        lax.fori_loop(0, nodes - 1, chunk, (jnp.int32(0), jnp.int32(0)))
 
         lane = lax.broadcasted_iota(jnp.int32, (ROWS * line, PAD), 1)
         for h in range(heads):
-            for p in (2 * h, 2 * h + 1):
-                way = 0 if p < pieces // 2 else 1
-                to(way, 0, p, own.at[p], half - 1).wait_recv()
-            attend(h, [opposite[2 * h]], [opposite[2 * h + 1]])
             total = totals[h]
             high = total.astype(bf16)
             low = (total - high.astype(f32)).astype(bf16)
@@ -324,17 +374,16 @@
 
     @pl.when(on_ring)
     def _():
-        def sent(step, carry):
-            for way in range(2):
+        for way in range(2):
+
+            def sent(step, carry):
                 for p in range(pieces):
                     pltpu.make_async_copy(
                         ring.at[way, step, p], ring.at[way, step, p], ring_send.at[way, step, p]
                     ).wait()
-            return carry
-
-        lax.fori_loop(0, half - 1, sent, 0)
-        for p in range(pieces):
-            pltpu.make_async_copy(opposite.at[p], opposite.at[p], far_send.at[p]).wait()
+                return carry
+
+            lax.fori_loop(0, most[way], sent, 0)
         for r, d, c in backs:
             if (r, d, c) != (0, 0, 0):
                 give_back(r, d, c).wait_send()
@@ -344,8 +393,8 @@
     tokens, width = query.shape
     heads = width // HD // COLUMNS
     nodes = lines // ROWS
-    half = nodes // 2
     pieces = 2 * heads
+    most = max(AHEAD, nodes - 1 - AHEAD)
     line = 2 * COLUMNS * tokens
     window = 3 * PAD
     f32, bf16 = jnp.float32, jnp.bfloat16
@@ -365,8 +414,7 @@
             pltpu.VMEM((2, window, line), f32),
             pltpu.VMEM((PAD, PAD), f32),
             pltpu.VMEM((pieces, HD, line), bf16),
-            pltpu.VMEM((pieces, HD, line), bf16),
-            pltpu.VMEM((2, half - 1, pieces, HD, line), bf16),
+            pltpu.VMEM((2, most, pieces, HD, line), bf16),
             pltpu.VMEM((heads, ROWS * line, PAD), bf16),
             pltpu.VMEM((heads, ROWS * line, PAD), f32),
             pltpu.VMEM((ROWS * line, heads * PAD), bf16),
@@ -375,13 +423,12 @@
             dma((3,)),
             dma(((2 + ROWS) * COLUMNS,)),
             dma((2 + ROWS,)),
-            dma((2, half - 1, pieces)),
-            dma((2, half - 1, pieces)),
-            dma((pieces,)),
-            dma((pieces,)),
+            dma((2, most, pieces)),
+            dma((2, most, pieces)),
             dma((ROWS * COLUMNS * 2,)),
             dma((ROWS * COLUMNS,)),
             dma((3,)),
+            pltpu.SemaphoreType.REGULAR((2,)),
         ],
         compiler_params=pltpu.CompilerParams(collective_id=0, has_side_effects=True),
         name="attention",

time: 92.3 us -> 124 us (1.34)
  Pallas kernels: 90.5 us -> 122 us
    pallas_call x1, Pallas kernels: 90.5 us -> 122 us  [on_device(): pl.pallas_call(functools.partial(kernel, nodes, heads), out_shape=jax.Sha...]
where the time goes in v2:
time: 124 us
  Pallas kernels  122 us (98%)
  local copies, waits for them, and re-layouts  1.52 us (1%)
    pallas_call x1, Pallas kernels, on_device(): pl.pallas_call(functools.partial(kernel, nodes, heads), out_shape=jax.Sha...  122 us

profile of v2, /device:TPU:33, one launch (start us, length us, event | category | flops | bytes accessed | tf_op | source)
XLA Modules:
  0.0 123.8 jit_solution(16257639945016672253)
XLA Ops:
  0.0 122.2 %attention.1 = bf16[16,2304]{1,0:T(8,128)(2,1)} custom-call(bf16[16,1152]{1,0:T(8,128)(2,1)} %query.1, bf16[16,1152]{1,0:T(8,128)(2,1)} %key.1, bf16[16,1152]{1,0:T(8,128)(2,1)} %value.1, f32[1,96]{1,0:T(1,128)} %bitcast.2, f32[1,96]{1,0:T(1,128)} %bitcast.3, bf16[576,2304]{1,0:T(8,128)(2,1)} %weight.1), custom_call_target="tpu_custom_call" | custom-call | tf_op jit(solution)/shard_map/attention/pallas_call | solution.py:404
  122.2 1.5 %copy.8 = bf16[16,2304]{1,0:T(8,128)(2,1)} copy(bf16[16,2304]{1,0:T(8,128)(2,1)} %attention.1) | data formatting | bytes 147456

commit v3 on v1

v3 whole, which is shorter than its diff:
```python
import functools
import math

import jax
import jax.numpy as jnp
from jax import lax
from jax.experimental import pallas as pl
from jax.experimental.pallas import tpu as pltpu
from jax.sharding import PartitionSpec as P

HD = 96
PAD = 128
COLUMNS = 4
ROWS = 2
FEED_CORE = 1
AHEAD = 6
MESH = pl.DeviceIdType.MESH
TN = (((1,), (1,)), ((), ()))


def kernel(
    nodes,
    heads,
    query,
    key,
    value,
    q_gain,
    k_gain,
    weight,
    mixed,
    stage,
    key_raw,
    value_raw,
    query_raw,
    turned,
    gain_pad,
    own,
    ring,
    q_heads,
    totals,
    parts_out,
    parts_in,
    whole_weight,
    stage_sem,
    feed_send,
    feed_recv,
    ring_send,
    ring_recv,
    back_send,
    back_recv,
    weight_sem,
    pair_send,
    pair_recv,
    ready,
):
    f32, bf16 = jnp.float32, jnp.bfloat16
    block = lax.axis_index("blk")
    core = lax.axis_index("uly")
    z, x = lax.div(block, COLUMNS), lax.rem(block, COLUMNS)
    z_block, z_row = lax.div(z, ROWS), lax.rem(z, ROWS)
    feeds_pair = core == FEED_CORE
    tokens = query.shape[0]
    window = 3 * PAD
    lanes = 2 * PAD
    group = heads * HD
    line = 2 * COLUMNS * tokens
    pieces = 2 * heads
    steps = jnp.where(feeds_pair, nodes - 1 - AHEAD, AHEAD)

    def device(row, column, a_core):
        return {"blk": row * COLUMNS + column, "uly": a_core}

    def other_row(r):
        return z_block * ROWS + lax.rem(z_row + r, ROWS)

    def other_column(d):
        return lax.rem(x + d, COLUMNS)

    node, last_node = z_block, nodes - 1
    ahead = lax.rem(z + ROWS, nodes * ROWS)
    behind = lax.rem(z + last_node * ROWS, nodes * ROWS)
    is_first, is_last = node == 0, node == last_node

    staged = [
        pltpu.make_async_copy(src, stage.at[i], stage_sem.at[i])
        for i, src in enumerate((key, value, query))
    ]
    for copy in staged:
        copy.start()

    barrier = pltpu.get_barrier_semaphore()

    def greet(dev):
        pl.semaphore_signal(barrier, inc=1, device_id=dev, device_id_type=MESH)

    for r in range(ROWS):
        for d in range(COLUMNS):
            for c in range(2):
                if (r, d, c) != (0, 0, 0):
                    greet(device(other_row(r), other_column(d), lax.rem(core + c, 2)))

    @pl.when(jnp.logical_not(is_last))
    def _():
        greet(device(ahead, x, core))

    @pl.when(is_first)
    def _():
        greet(device(behind, x, core))

    lower = jnp.where(is_first, 0, 1) + jnp.where(is_last, 1, 0)
    pl.semaphore_wait(barrier, 2 * ROWS * COLUMNS - 1 + lower)

    target = jnp.where(feeds_pair, behind, ahead)
    source = jnp.where(feeds_pair, ahead, behind)

    @pl.when(jnp.where(feeds_pair, node == last_node, node != 0))
    def _():
        pl.semaphore_signal(ready, inc=1, device_id=device(source, x, core), device_id_type=MESH)

    def wait_for_target():
        @pl.when(jnp.where(feeds_pair, node == 0, node != last_node))
        def _():
            pl.semaphore_wait(ready, 1)

    place = pl.ds(pl.multiple_of((x * 2 + core) * tokens, tokens), tokens)

    def feed(i, r, d):
        column = other_column(d)
        dst = (key_raw, value_raw, query_raw.at[z_row])[i].at[place]
        recv = feed_recv.at[i] if i < 2 else feed_recv.at[2 + z_row]
        return pltpu.make_async_remote_copy(
            src_ref=stage.at[i, :, pl.ds(pl.multiple_of(column * lanes, PAD), window)],
            dst_ref=dst,
            send_sem=feed_send.at[i * COLUMNS + d if i < 2 else (2 + r) * COLUMNS + d],
            recv_sem=recv,
            device_id=device(other_row(r), column, FEED_CORE),
            device_id_type=MESH,
        )

    def own_feed(i):
        dst = (key_raw, value_raw, query_raw.at[z_row])[i].at[place]
        recv = feed_recv.at[i] if i < 2 else feed_recv.at[2 + z_row]
        src = (key, value, query)[i]
        return pltpu.make_async_copy(
            src.at[:, pl.ds(pl.multiple_of(x * lanes, PAD), window)], dst, recv
        )

    feeds = [(i, r, d) for i in range(3) for r in range(ROWS if i == 2 else 1) for d in (2, 1, 3, 0)]
    for i, r, d in feeds:
        if (r, d) == (0, 2):
            staged[i].wait()
        if (r, d) == (0, 0):

            @pl.when(feeds_pair)
            def _():
                own_feed(i).start()

            @pl.when(core != FEED_CORE)
            def _():
                feed(i, r, d).start()

        else:
            feed(i, r, d).start()

    depth = weight.shape[0]
    mine = whole_weight.at[pl.ds(pl.multiple_of(core * depth, 16), depth)]
    local_weight = pltpu.make_async_copy(weight, mine, weight_sem.at[0])
    sent_weight = pltpu.make_async_remote_copy(
        src_ref=weight,
        dst_ref=mine,
        send_sem=weight_sem.at[1],
        recv_sem=weight_sem.at[2],
        device_id=device(z, x, 1 - core),
        device_id_type=MESH,
    )
    local_weight.start()
    sent_weight.start()

    def give_back(r, d, c):
        column, a_core = other_column(d), lax.rem(core + c, 2)
        row = lax.rem(z_row + r, ROWS)
        start = row * line + (column * 2 + a_core) * tokens
        return pltpu.make_async_remote_copy(
            src_ref=parts_out.at[pl.ds(pl.multiple_of(start, tokens), tokens)],
            dst_ref=parts_in.at[core, z_row, x],
            send_sem=back_send.at[(r * COLUMNS + d) * 2 + c],
            recv_sem=back_recv.at[(core * ROWS + z_row) * COLUMNS + x],
            device_id=device(other_row(r), column, a_core),
            device_id_type=MESH,
        )

    backs = [(r, d, c) for r in range(ROWS) for d in range(COLUMNS) for c in range(2)]

    def landing(step, p, src):
        return pltpu.make_async_remote_copy(
            src_ref=src,
            dst_ref=ring.at[step, p],
            send_sem=ring_send.at[step],
            recv_sem=ring_recv.at[step, p],
            device_id=device(target, x, core),
            device_id_type=MESH,
        )

    def to_pair(ref, p):
        return pltpu.make_async_remote_copy(
            src_ref=ref,
            dst_ref=ref,
            send_sem=pair_send.at[p],
            recv_sem=pair_recv.at[p],
            device_id=device(z, x, 1 - core),
            device_id_type=MESH,
        )

    scale = float(HD) ** (-0.5) * math.log2(math.e)

    def attend(h, k, v):
        k = jnp.concatenate([k, jnp.zeros((PAD - HD, line), bf16)], axis=0)
        v = jnp.concatenate([v, jnp.ones((PAD - HD, line), bf16)], axis=0)
        scores = jnp.dot(q_heads[h], k, preferred_element_type=f32)
        expd = jnp.exp2(scores * scale).astype(bf16)
        totals[h] += lax.dot_general(expd, v, TN, preferred_element_type=f32)

    totals[...] = jnp.zeros_like(totals)

    @pl.when(feeds_pair)
    def _():
        for i, gain in enumerate((q_gain, k_gain)):
            gain_pad[...] = jnp.zeros_like(gain_pad)
            gain_pad[:, 0:HD] = jnp.broadcast_to(gain[...], (PAD, HD))
            turned[i, 0:PAD, :] = gain_pad[...].T
        q_column, k_column = turned[0, 0:HD, :], turned[1, 0:HD, :]
        first = x * (group - lanes)

        def head_of(i, h):
            return turned[i, pl.ds(pl.multiple_of(first + h * HD, 32), HD), :]

        def normed(data, gain):
            meansq = jnp.mean(data * data, axis=0, keepdims=True)
            return data * lax.rsqrt(meansq + 1e-06) * gain

        pltpu.make_async_copy(key_raw, key_raw, feed_recv.at[0]).wait()
        turned[0] = key_raw[...].astype(f32).T
        for h in range(heads):
            own[2 * h] = normed(head_of(0, h), k_column).astype(bf16)
        pltpu.make_async_copy(value_raw, value_raw, feed_recv.at[1]).wait()
        turned[1] = value_raw[...].astype(f32).T
        for h in range(heads):
            own[2 * h + 1] = head_of(1, h).astype(bf16)

        @pl.when(node != 0)
        def _():
            for p in range(pieces):
                landing(0, p, own.at[p]).start()

        for p in range(pieces):
            to_pair(own.at[p], p).start()

        for r in range(ROWS):
            rows = query_raw.at[r]
            pltpu.make_async_copy(rows, rows, feed_recv.at[2 + r]).wait()
            turned[0] = query_raw[r].astype(f32).T
            for h in range(heads):
                data = normed(head_of(0, h), q_column)
                data = jnp.concatenate([data, jnp.zeros((PAD - HD, line), f32)], axis=0)
                q_heads[h, r * line : (r + 1) * line, :] = data.T.astype(bf16)

        for h in range(heads):
            to_pair(q_heads.at[h], pieces + h).start()
        for h in range(heads):
            attend(h, own[2 * h], own[2 * h + 1])
        wait_for_target()

        @pl.when(node == 0)
        def _():
            for p in range(pieces):
                landing(0, p, own.at[p]).start()

    @pl.when(core != FEED_CORE)
    def _():
        wait_for_target()
        for p in range(pieces):
            to_pair(own.at[p], p).wait_recv()
            landing(0, p, own.at[p]).start()
        for h in range(heads):
            to_pair(q_heads.at[h], pieces + h).wait_recv()

    def chunk(step, carry):
        for h in range(heads):
            for p in (2 * h, 2 * h + 1):
                landing(step, p, own.at[p]).wait_recv()

                @pl.when(step < steps - 1)
                def _():
                    landing(step + 1, p, ring.at[step, p]).start()

            attend(h, ring[step, 2 * h], ring[step, 2 * h + 1])
        return carry

    lax.fori_loop(0, steps, chunk, 0)

    lane = lax.broadcasted_iota(jnp.int32, (ROWS * line, PAD), 1)
    for h in range(heads):
        total = totals[h]
        high = total.astype(bf16)
        low = (total - high.astype(f32)).astype(bf16)
        parts_out[:, h * PAD : (h + 1) * PAD] = jnp.where(lane >= HD + 16, low, high)

    for r, d, c in backs:
        if (r, d, c) != (0, 0, 0):
            give_back(r, d, c).start()
    own_start = z_row * line + (x * 2 + core) * tokens
    parts_in[core, z_row, x] = parts_out[pl.ds(pl.multiple_of(own_start, tokens), tokens)]

    for i, r, d in feeds:
        if (r, d) == (0, 0):

            @pl.when(core != FEED_CORE)
            def _():
                feed(i, r, d).wait_send()

        else:
            feed(i, r, d).wait_send()

    @pl.when(feeds_pair)
    def _():
        for p in range(pieces):
            to_pair(own.at[p], p).wait_send()
        for h in range(heads):
            to_pair(q_heads.at[h], pieces + h).wait_send()

    def sent(step, carry):
        pltpu.make_async_copy(ring.at[step], ring.at[step], ring_send.at[step]).wait()
        return carry

    lax.fori_loop(0, steps, sent, 0)
    for r, d, c in backs:
        if (r, d, c) != (0, 0, 0):
            give_back(r, d, c).wait_send()

    local_weight.wait()
    sent_weight.wait()
    attn = []
    sources = [(c, r, d) for c in range(2) for r in range(ROWS) for d in range(COLUMNS)]
    for i, (c, r, d) in enumerate(sources):
        itself = (z_row == r) & (x == d) & (core == c)

        @pl.when(jnp.logical_not(itself))
        def _():
            part = parts_in.at[c, r, d]
            pltpu.make_async_copy(part, part, back_recv.at[i]).wait()

    for d in range(COLUMNS):
        for h in range(heads):
            part = sum(
                parts_in[c, r, d, :, h * PAD : (h + 1) * PAD].astype(f32)
                for c in range(2)
                for r in range(ROWS)
            )
            total_weight = part[:, HD : HD + 1] + part[:, HD + 16 : HD + 17]
            attn.append((part[:, 0:HD] / total_weight).astype(bf16))
    attn = jnp.concatenate(attn, axis=1)
    mixed[...] = jnp.dot(attn, whole_weight[...], preferred_element_type=f32).astype(bf16)


def on_device(lines, query, key, value, q_gain, k_gain, out_weight):
    tokens, width = query.shape
    heads = width // HD // COLUMNS
    nodes = lines // ROWS
    pieces = 2 * heads
    most = max(AHEAD, nodes - 1 - AHEAD)
    line = 2 * COLUMNS * tokens
    window = 3 * PAD
    f32, bf16 = jnp.float32, jnp.bfloat16
    hbm = pl.BlockSpec(memory_space=pl.ANY)
    vmem = pl.BlockSpec(memory_space=pltpu.VMEM)
    dma = pltpu.SemaphoreType.DMA
    return pl.pallas_call(
        functools.partial(kernel, nodes, heads),
        out_shape=jax.ShapeDtypeStruct((tokens, out_weight.shape[1]), bf16),
        in_specs=[hbm, hbm, hbm, vmem, vmem, hbm],
        out_specs=vmem,
        scratch_shapes=[
            pltpu.VMEM((3, tokens, width), bf16),
            pltpu.VMEM((line, window), bf16),
            pltpu.VMEM((line, window), bf16),
            pltpu.VMEM((ROWS, line, window), bf16),
            pltpu.VMEM((2, window, line), f32),
            pltpu.VMEM((PAD, PAD), f32),
            pltpu.VMEM((pieces, HD, line), bf16),
            pltpu.VMEM((most, pieces, HD, line), bf16),
            pltpu.VMEM((heads, ROWS * line, PAD), bf16),
            pltpu.VMEM((heads, ROWS * line, PAD), f32),
            pltpu.VMEM((ROWS * line, heads * PAD), bf16),
            pltpu.VMEM((2, ROWS, COLUMNS, tokens, heads * PAD), bf16),
            pltpu.VMEM((2 * out_weight.shape[0], out_weight.shape[1]), bf16),
            dma((3,)),
            dma(((2 + ROWS) * COLUMNS,)),
            dma((2 + ROWS,)),
            dma((most,)),
            dma((most, pieces)),
            dma((ROWS * COLUMNS * 2,)),
            dma((2 * ROWS * COLUMNS,)),
            dma((3,)),
            dma((pieces + heads,)),
            dma((pieces + heads,)),
            pltpu.SemaphoreType.REGULAR,
        ],
        compiler_params=pltpu.CompilerParams(collective_id=0, has_side_effects=True),
        name="attention",
    )(query, key, value, q_gain.reshape(1, HD), k_gain.reshape(1, HD), out_weight)


def solution(mesh):
    tokens = P(("grp", "blk", "uly"), None)
    return jax.shard_map(
        functools.partial(on_device, mesh.shape["blk"] // COLUMNS),
        mesh=mesh,
        in_specs=(tokens, tokens, tokens, P(), P(), P("uly", None)),
        out_specs=tokens,
        check_vma=False,
    )
```

time: 92.3 us -> 87.8 us (0.951)
  Pallas kernels: 90.5 us -> 86 us
    pallas_call x1, Pallas kernels: 90.5 us -> 86 us  [on_device(): pl.pallas_call(functools.partial(kernel, nodes, heads), out_shape=jax.Sha...]
where the time goes in v3:
time: 87.8 us; the launch traced here: 87.5 us
  Pallas kernels  86 us (98%)
  local copies, waits for them, and re-layouts  1.52 us (2%)
    pallas_call x1, Pallas kernels, on_device(): pl.pallas_call(functools.partial(kernel, nodes, heads), out_shape=jax.Sha...  86 us

profile of v3, /device:TPU:33, one launch (start us, length us, event | category | flops | bytes accessed | tf_op | source)
XLA Modules:
  0.0 87.5 jit_solution(6131643811508153333)
XLA Ops:
  0.0 86.0 %attention.1 = bf16[16,2304]{1,0:T(8,128)(2,1)} custom-call(bf16[16,1152]{1,0:T(8,128)(2,1)} %query.1, bf16[16,1152]{1,0:T(8,128)(2,1)} %key.1, bf16[16,1152]{1,0:T(8,128)(2,1)} %value.1, f32[1,96]{1,0:T(1,128)} %bitcast.2, f32[1,96]{1,0:T(1,128)} %bitcast.3, bf16[576,2304]{1,0:T(8,128)(2,1)} %weight.1), custom_call_target="tpu_custom_call" | custom-call | tf_op jit(solution)/shard_map/attention/pallas_call | solution.py:377
  86.0 1.5 %copy.8 = bf16[16,2304]{1,0:T(8,128)(2,1)} copy(bf16[16,2304]{1,0:T(8,128)(2,1)} %attention.1) | data formatting | bytes 147456

commit v4 on v3

--- a/solution.py
+++ b/solution.py
@@ -13,7 +13,7 @@
 COLUMNS = 4
 ROWS = 2
 FEED_CORE = 1
-AHEAD = 6
+AHEAD = 5
 MESH = pl.DeviceIdType.MESH
 TN = (((1,), (1,)), ((), ()))
 
@@ -33,6 +33,7 @@
     value_raw,
     query_raw,
     turned,
+    gain_rows,
     gain_pad,
     own,
     ring,
@@ -42,6 +43,7 @@
     parts_in,
     whole_weight,
     stage_sem,
+    gain_sem,
     feed_send,
     feed_recv,
     ring_send,
@@ -85,7 +87,11 @@
         pltpu.make_async_copy(src, stage.at[i], stage_sem.at[i])
         for i, src in enumerate((key, value, query))
     ]
-    for copy in staged:
+    gains = [
+        pltpu.make_async_copy(src, gain_rows.at[i], gain_sem.at[i])
+        for i, src in enumerate((q_gain, k_gain))
+    ]
+    for copy in staged + gains:
         copy.start()
 
     barrier = pltpu.get_barrier_semaphore()
@@ -93,32 +99,37 @@
     def greet(dev):
         pl.semaphore_signal(barrier, inc=1, device_id=dev, device_id_type=MESH)
 
-    for r in range(ROWS):
-        for d in range(COLUMNS):
-            for c in range(2):
-                if (r, d, c) != (0, 0, 0):
-                    greet(device(other_row(r), other_column(d), lax.rem(core + c, 2)))
-
-    @pl.when(jnp.logical_not(is_last))
+    @pl.when(feeds_pair)
+    def _():
+        for r in range(ROWS):
+            for d in range(COLUMNS):
+                for c in range(2):
+                    if (r, d, c) != (0, 0, 0):
+                        greet(device(other_row(r), other_column(d), lax.rem(core + c, 2)))
+
+    greets_ahead = jnp.where(feeds_pair, node != last_node, (node != 0) & (node != last_node))
+    greets_behind = jnp.where(feeds_pair, node == 0, node < 2)
+    lower = jnp.where(feeds_pair, node != 0, node != 1).astype(jnp.int32) + jnp.where(is_last, 1, 0)
+
+    @pl.when(greets_ahead)
     def _():
         greet(device(ahead, x, core))
 
-    @pl.when(is_first)
+    @pl.when(greets_behind)
     def _():
         greet(device(behind, x, core))
 
-    lower = jnp.where(is_first, 0, 1) + jnp.where(is_last, 1, 0)
-    pl.semaphore_wait(barrier, 2 * ROWS * COLUMNS - 1 + lower)
+    pl.semaphore_wait(barrier, ROWS * COLUMNS - jnp.where(feeds_pair, 1, 0) + lower)
 
     target = jnp.where(feeds_pair, behind, ahead)
     source = jnp.where(feeds_pair, ahead, behind)
 
-    @pl.when(jnp.where(feeds_pair, node == last_node, node != 0))
+    @pl.when(jnp.where(feeds_pair, node == last_node, node > 1))
     def _():
         pl.semaphore_signal(ready, inc=1, device_id=device(source, x, core), device_id_type=MESH)
 
     def wait_for_target():
-        @pl.when(jnp.where(feeds_pair, node == 0, node != last_node))
+        @pl.when(jnp.where(feeds_pair, node == 0, (node != 0) & (node != last_node)))
         def _():
             pl.semaphore_wait(ready, 1)
 
@@ -174,16 +185,19 @@
         device_id_type=MESH,
     )
     local_weight.start()
-    sent_weight.start()
-
-    def give_back(r, d, c):
+
+    @pl.when(core != FEED_CORE)
+    def _():
+        sent_weight.start()
+
+    def give_back(r, d, c, h):
         column, a_core = other_column(d), lax.rem(core + c, 2)
         row = lax.rem(z_row + r, ROWS)
         start = row * line + (column * 2 + a_core) * tokens
         return pltpu.make_async_remote_copy(
-            src_ref=parts_out.at[pl.ds(pl.multiple_of(start, tokens), tokens)],
-            dst_ref=parts_in.at[core, z_row, x],
-            send_sem=back_send.at[(r * COLUMNS + d) * 2 + c],
+            src_ref=parts_out.at[h, pl.ds(pl.multiple_of(start, tokens), tokens)],
+            dst_ref=parts_in.at[core, z_row, x, h],
+            send_sem=back_send.at[h],
             recv_sem=back_recv.at[(core * ROWS + z_row) * COLUMNS + x],
             device_id=device(other_row(r), column, a_core),
             device_id_type=MESH,
@@ -224,9 +238,10 @@
 
     @pl.when(feeds_pair)
     def _():
-        for i, gain in enumerate((q_gain, k_gain)):
+        for i in range(2):
+            gains[i].wait()
             gain_pad[...] = jnp.zeros_like(gain_pad)
-            gain_pad[:, 0:HD] = jnp.broadcast_to(gain[...], (PAD, HD))
+            gain_pad[:, 0:HD] = jnp.broadcast_to(gain_rows[i], (PAD, HD))
             turned[i, 0:PAD, :] = gain_pad[...].T
         q_column, k_column = turned[0, 0:HD, :], turned[1, 0:HD, :]
         first = x * (group - lanes)
@@ -238,22 +253,25 @@
             meansq = jnp.mean(data * data, axis=0, keepdims=True)
             return data * lax.rsqrt(meansq + 1e-06) * gain
 
+        def send_own(kind):
+            for p in range(kind * heads, (kind + 1) * heads):
+
+                @pl.when(node != 0)
+                def _():
+                    landing(0, p, own.at[p]).start()
+
+                to_pair(own.at[p], p).start()
+
         pltpu.make_async_copy(key_raw, key_raw, feed_recv.at[0]).wait()
         turned[0] = key_raw[...].astype(f32).T
         for h in range(heads):
-            own[2 * h] = normed(head_of(0, h), k_column).astype(bf16)
+            own[h] = normed(head_of(0, h), k_column).astype(bf16)
+        send_own(0)
         pltpu.make_async_copy(value_raw, value_raw, feed_recv.at[1]).wait()
         turned[1] = value_raw[...].astype(f32).T
         for h in range(heads):
-            own[2 * h + 1] = head_of(1, h).astype(bf16)
-
-        @pl.when(node != 0)
-        def _():
-            for p in range(pieces):
-                landing(0, p, own.at[p]).start()
-
-        for p in range(pieces):
-            to_pair(own.at[p], p).start()
+            own[heads + h] = head_of(1, h).astype(bf16)
+        send_own(1)
 
         for r in range(ROWS):
             rows = query_raw.at[r]
@@ -266,8 +284,9 @@
 
         for h in range(heads):
             to_pair(q_heads.at[h], pieces + h).start()
-        for h in range(heads):
-            attend(h, own[2 * h], own[2 * h + 1])
+        sent_weight.start()
+        for h in range(heads):
+            attend(h, own[h], own[heads + h])
         wait_for_target()
 
         @pl.when(node == 0)
@@ -277,6 +296,8 @@
 
     @pl.when(core != FEED_CORE)
     def _():
+        for copy in gains:
+            copy.wait()
         wait_for_target()
         for p in range(pieces):
             to_pair(own.at[p], p).wait_recv()
@@ -284,32 +305,34 @@
         for h in range(heads):
             to_pair(q_heads.at[h], pieces + h).wait_recv()
 
+    lane = lax.broadcasted_iota(jnp.int32, (ROWS * line, PAD), 1)
+
+    def ring_step(step, last):
+        for p in range(pieces):
+            landing(step, p, own.at[p]).wait_recv()
+            if not last:
+                landing(step + 1, p, ring.at[step, p]).start()
+            if p >= heads:
+                h = p - heads
+                attend(h, ring[step, h], ring[step, p])
+                if last:
+                    total = totals[h]
+                    high = total.astype(bf16)
+                    low = (total - high.astype(f32)).astype(bf16)
+                    parts_out[h] = jnp.where(lane >= HD + 16, low, high)
+                    for r, d, c in backs:
+                        if (r, d, c) != (0, 0, 0):
+                            give_back(r, d, c, h).start()
+
     def chunk(step, carry):
-        for h in range(heads):
-            for p in (2 * h, 2 * h + 1):
-                landing(step, p, own.at[p]).wait_recv()
-
-                @pl.when(step < steps - 1)
-                def _():
-                    landing(step + 1, p, ring.at[step, p]).start()
-
-            attend(h, ring[step, 2 * h], ring[step, 2 * h + 1])
+        ring_step(step, False)
         return carry
 
-    lax.fori_loop(0, steps, chunk, 0)
-
-    lane = lax.broadcasted_iota(jnp.int32, (ROWS * line, PAD), 1)
+    lax.fori_loop(0, steps - 1, chunk, 0)
+    ring_step(steps - 1, True)
+    own_start = z_row * line + (x * 2 + core) * tokens
     for h in range(heads):
-        total = totals[h]
-        high = total.astype(bf16)
-        low = (total - high.astype(f32)).astype(bf16)
-        parts_out[:, h * PAD : (h + 1) * PAD] = jnp.where(lane >= HD + 16, low, high)
-
-    for r, d, c in backs:
-        if (r, d, c) != (0, 0, 0):
-            give_back(r, d, c).start()
-    own_start = z_row * line + (x * 2 + core) * tokens
-    parts_in[core, z_row, x] = parts_out[pl.ds(pl.multiple_of(own_start, tokens), tokens)]
+        parts_in[core, z_row, x, h] = parts_out[h, pl.ds(pl.multiple_of(own_start, tokens), tokens)]
 
     for i, r, d in feeds:
         if (r, d) == (0, 0):
@@ -333,9 +356,9 @@
         return carry
 
     lax.fori_loop(0, steps, sent, 0)
-    for r, d, c in backs:
-        if (r, d, c) != (0, 0, 0):
-            give_back(r, d, c).wait_send()
+    for h in range(heads):
+        others = parts_out.at[h, 0 : (len(backs) - 1) * tokens]
+        pltpu.make_async_copy(others, others, back_send.at[h]).wait()
 
     local_weight.wait()
     sent_weight.wait()
@@ -352,7 +375,7 @@
     for d in range(COLUMNS):
         for h in range(heads):
             part = sum(
-                parts_in[c, r, d, :, h * PAD : (h + 1) * PAD].astype(f32)
+                parts_in[c, r, d, h].astype(f32)
                 for c in range(2)
                 for r in range(ROWS)
             )
@@ -377,7 +400,7 @@
     return pl.pallas_call(
         functools.partial(kernel, nodes, heads),
         out_shape=jax.ShapeDtypeStruct((tokens, out_weight.shape[1]), bf16),
-        in_specs=[hbm, hbm, hbm, vmem, vmem, hbm],
+        in_specs=[hbm] * 6,
         out_specs=vmem,
         scratch_shapes=[
             pltpu.VMEM((3, tokens, width), bf16),
@@ -385,20 +408,22 @@
             pltpu.VMEM((line, window), bf16),
             pltpu.VMEM((ROWS, line, window), bf16),
             pltpu.VMEM((2, window, line), f32),
+            pltpu.VMEM((2, 1, HD), f32),
             pltpu.VMEM((PAD, PAD), f32),
             pltpu.VMEM((pieces, HD, line), bf16),
             pltpu.VMEM((most, pieces, HD, line), bf16),
             pltpu.VMEM((heads, ROWS * line, PAD), bf16),
             pltpu.VMEM((heads, ROWS * line, PAD), f32),
-            pltpu.VMEM((ROWS * line, heads * PAD), bf16),
-            pltpu.VMEM((2, ROWS, COLUMNS, tokens, heads * PAD), bf16),
+            pltpu.VMEM((heads, ROWS * line, PAD), bf16),
+            pltpu.VMEM((2, ROWS, COLUMNS, heads, tokens, PAD), bf16),
             pltpu.VMEM((2 * out_weight.shape[0], out_weight.shape[1]), bf16),
             dma((3,)),
+            dma((2,)),
             dma(((2 + ROWS) * COLUMNS,)),
             dma((2 + ROWS,)),
             dma((most,)),
             dma((most, pieces)),
-            dma((ROWS * COLUMNS * 2,)),
+            dma((heads,)),
             dma((2 * ROWS * COLUMNS,)),
             dma((3,)),
             dma((pieces + heads,)),

time: 87.8 us -> 90.1 us (1.026)
  Pallas kernels: 86 us -> 88.3 us
    pallas_call x1, Pallas kernels: 86 us -> 88.3 us  [on_device(): pl.pallas_call(functools.partial(kernel, nodes, heads), out_shape=jax.Sha...]
where the time goes in v4:
time: 90.1 us; the launch traced here: 89.9 us
  Pallas kernels  88.3 us (98%)
  local copies, waits for them, and re-layouts  1.52 us (2%)
    pallas_call x1, Pallas kernels, on_device(): pl.pallas_call(functools.partial(kernel, nodes, heads), out_shape=jax.Sha...  88.3 us

profile of v4, /device:TPU:33, one launch (start us, length us, event | category | flops | bytes accessed | tf_op | source)
XLA Modules:
  0.0 89.9 jit_solution(14300684978305706263)
XLA Ops:
  0.0 88.3 %attention.1 = bf16[16,2304]{1,0:T(8,128)(2,1)} custom-call(bf16[16,1152]{1,0:T(8,128)(2,1)} %query.1, bf16[16,1152]{1,0:T(8,128)(2,1)} %key.1, bf16[16,1152]{1,0:T(8,128)(2,1)} %value.1, f32[1,96]{1,0:T(1,128)} %bitcast.2, f32[1,96]{1,0:T(1,128)} %bitcast.3, bf16[576,2304]{1,0:T(8,128)(2,1)} %weight.1), custom_call_target="tpu_custom_call" | custom-call | tf_op jit(solution)/shard_map/attention/pallas_call | solution.py:400
  88.4 1.5 %copy.8 = bf16[16,2304]{1,0:T(8,128)(2,1)} copy(bf16[16,2304]{1,0:T(8,128)(2,1)} %attention.1) | data formatting | bytes 147456

commit v5 on v4

--- a/solution.py
+++ b/solution.py
@@ -13,7 +13,8 @@
 COLUMNS = 4
 ROWS = 2
 FEED_CORE = 1
-AHEAD = 5
+UP = 5
+LAND = 3
 MESH = pl.DeviceIdType.MESH
 TN = (((1,), (1,)), ((), ()))
 
@@ -48,6 +49,8 @@
     feed_recv,
     ring_send,
     ring_recv,
+    also_send,
+    express_send,
     back_send,
     back_recv,
     weight_sem,
@@ -67,7 +70,8 @@
     group = heads * HD
     line = 2 * COLUMNS * tokens
     pieces = 2 * heads
-    steps = jnp.where(feeds_pair, nodes - 1 - AHEAD, AHEAD)
+    half = nodes // 2
+    far = half - UP
 
     def device(row, column, a_core):
         return {"blk": row * COLUMNS + column, "uly": a_core}
@@ -82,6 +86,32 @@
     ahead = lax.rem(z + ROWS, nodes * ROWS)
     behind = lax.rem(z + last_node * ROWS, nodes * ROWS)
     is_first, is_last = node == 0, node == last_node
+    is_low = node < half
+    express = feeds_pair & (node >= half) & (node < half + far)
+
+    steps = jnp.where(
+        feeds_pair,
+        jnp.where(node <= LAND, half + far - 1 - node, jnp.where(is_low, half - 1 - node, half)),
+        jnp.where(node <= LAND, node + UP, jnp.where(is_low, node + half, half - 1)),
+    )
+
+    def passes(slot):
+        owner = lax.rem(node + 1 + slot, nodes)
+        down = jnp.where(
+            owner < half, slot + 2 <= half, (node > half) | ((node <= LAND) & (node >= 1))
+        )
+        low_owner = slot < node
+        up = jnp.where(
+            is_low,
+            jnp.where(node + 1 < half, True, low_owner & (slot + 2 <= half - 1)),
+            jnp.where(is_last, slot + 2 <= UP, slot + 2 <= half - 1),
+        )
+        skip = jnp.where(~feeds_pair & (node == LAND) & (slot >= node), far, 0)
+        return jnp.where(feeds_pair, down, up), slot + 1 + skip
+
+    def passes_over(slot):
+        owner = node + 1 + slot
+        return feeds_pair & (node == LAND) & (owner >= half), owner - half + LAND + 1
 
     staged = [
         pltpu.make_async_copy(src, stage.at[i], stage_sem.at[i])
@@ -110,6 +140,7 @@
     greets_ahead = jnp.where(feeds_pair, node != last_node, (node != 0) & (node != last_node))
     greets_behind = jnp.where(feeds_pair, node == 0, node < 2)
     lower = jnp.where(feeds_pair, node != 0, node != 1).astype(jnp.int32) + jnp.where(is_last, 1, 0)
+    lower = lower + jnp.where(express, 1, 0)
 
     @pl.when(greets_ahead)
     def _():
@@ -118,6 +149,11 @@
     @pl.when(greets_behind)
     def _():
         greet(device(behind, x, core))
+
+    @pl.when(feeds_pair & (node == LAND))
+    def _():
+        for i in range(far):
+            greet(device((half + i) * ROWS + z_row, x, core))
 
     pl.semaphore_wait(barrier, ROWS * COLUMNS - jnp.where(feeds_pair, 1, 0) + lower)
 
@@ -205,14 +241,33 @@
 
     backs = [(r, d, c) for r in range(ROWS) for d in range(COLUMNS) for c in range(2)]
 
-    def landing(step, p, src):
+    most = ring.shape[0]
+
+    def landing(src, p, slot, dev, send_sem):
         return pltpu.make_async_remote_copy(
-            src_ref=src,
-            dst_ref=ring.at[step, p],
-            send_sem=ring_send.at[step],
-            recv_sem=ring_recv.at[step, p],
-            device_id=device(target, x, core),
+            src_ref=src.at[p],
+            dst_ref=ring.at[slot, p],
+            send_sem=send_sem,
+            recv_sem=ring_recv.at[slot, p],
+            device_id=dev,
             device_id_type=MESH,
+        )
+
+    def own_on(p):
+        return landing(own, p, 0, device(target, x, core), ring_send.at[most])
+
+    def own_express(p):
+        there = device(LAND * ROWS + z_row, x, core)
+        return landing(own, p, node - LAND - 1, there, express_send)
+
+    def passed(p, slot):
+        return landing(
+            ring.at[slot], p, passes(slot)[1], device(target, x, core), ring_send.at[slot]
+        )
+
+    def passed_over(p, slot):
+        return landing(
+            ring.at[slot], p, passes_over(slot)[1], device(ahead, x, 1 - core), also_send.at[slot]
         )
 
     def to_pair(ref, p):
@@ -254,12 +309,19 @@
             return data * lax.rsqrt(meansq + 1e-06) * gain
 
         def send_own(kind):
-            for p in range(kind * heads, (kind + 1) * heads):
-
-                @pl.when(node != 0)
-                def _():
-                    landing(0, p, own.at[p]).start()
-
+            mine = range(kind * heads, (kind + 1) * heads)
+
+            @pl.when(express)
+            def _():
+                for p in mine:
+                    own_express(p).start()
+
+            @pl.when((node != 0) & (node != half))
+            def _():
+                for p in mine:
+                    own_on(p).start()
+
+            for p in mine:
                 to_pair(own.at[p], p).start()
 
         pltpu.make_async_copy(key_raw, key_raw, feed_recv.at[0]).wait()
@@ -292,7 +354,7 @@
         @pl.when(node == 0)
         def _():
             for p in range(pieces):
-                landing(0, p, own.at[p]).start()
+                own_on(p).start()
 
     @pl.when(core != FEED_CORE)
     def _():
@@ -301,35 +363,54 @@
         wait_for_target()
         for p in range(pieces):
             to_pair(own.at[p], p).wait_recv()
-            landing(0, p, own.at[p]).start()
+            own_on(p).start()
         for h in range(heads):
             to_pair(q_heads.at[h], pieces + h).wait_recv()
 
     lane = lax.broadcasted_iota(jnp.int32, (ROWS * line, PAD), 1)
 
-    def ring_step(step, last):
+    def give(h):
+        total = totals[h]
+        high = total.astype(bf16)
+        low = (total - high.astype(f32)).astype(bf16)
+        parts_out[h] = jnp.where(lane >= HD + 16, low, high)
+        for r, d, c in backs:
+            if (r, d, c) != (0, 0, 0):
+                give_back(r, d, c, h).start()
+
+    def ring_step(slot, last):
         for p in range(pieces):
-            landing(step, p, own.at[p]).wait_recv()
-            if not last:
-                landing(step + 1, p, ring.at[step, p]).start()
+            landing(own, p, slot, device(target, x, core), ring_send.at[slot]).wait_recv()
+
+            @pl.when(passes(slot)[0])
+            def _():
+                passed(p, slot).start()
+
+            @pl.when(passes_over(slot)[0])
+            def _():
+                passed_over(p, slot).start()
+
             if p >= heads:
                 h = p - heads
-                attend(h, ring[step, h], ring[step, p])
+                attend(h, ring[slot, h], ring[slot, p])
                 if last:
-                    total = totals[h]
-                    high = total.astype(bf16)
-                    low = (total - high.astype(f32)).astype(bf16)
-                    parts_out[h] = jnp.where(lane >= HD + 16, low, high)
-                    for r, d, c in backs:
-                        if (r, d, c) != (0, 0, 0):
-                            give_back(r, d, c, h).start()
-
-    def chunk(step, carry):
-        ring_step(step, False)
+                    give(h)
+
+    def chunk(slot, carry):
+        ring_step(slot, False)
         return carry
 
     lax.fori_loop(0, steps - 1, chunk, 0)
-    ring_step(steps - 1, True)
+
+    @pl.when(steps > 0)
+    def _():
+        ring_step(steps - 1, True)
+
+    @pl.when(steps == 0)
+    def _():
+        for h in range(heads):
+            give(h)
+
     own_start = z_row * line + (x * 2 + core) * tokens
     for h in range(heads):
         parts_in[core, z_row, x, h] = parts_out[h, pl.ds(pl.multiple_of(own_start, tokens), tokens)]
@@ -351,8 +432,23 @@
         for h in range(heads):
             to_pair(q_heads.at[h], pieces + h).wait_send()
 
-    def sent(step, carry):
-        pltpu.make_async_copy(ring.at[step], ring.at[step], ring_send.at[step]).wait()
+    @pl.when(express)
+    def _():
+        pltpu.make_async_copy(own, own, express_send).wait()
+
+    @pl.when(jnp.logical_not(feeds_pair & (node == half)))
+    def _():
+        pltpu.make_async_copy(own, own, ring_send.at[most]).wait()
+
+    def sent(slot, carry):
+        @pl.when(passes(slot)[0])
+        def _():
+            pltpu.make_async_copy(ring.at[slot], ring.at[slot], ring_send.at[slot]).wait()
+
+        @pl.when(passes_over(slot)[0])
+        def _():
+            pltpu.make_async_copy(ring.at[slot], ring.at[slot], also_send.at[slot]).wait()
+
         return carry
 
     lax.fori_loop(0, steps, sent, 0)
@@ -390,7 +486,7 @@
     heads = width // HD // COLUMNS
     nodes = lines // ROWS
     pieces = 2 * heads
-    most = max(AHEAD, nodes - 1 - AHEAD)
+    most = nodes - 1
     line = 2 * COLUMNS * tokens
     window = 3 * PAD
     f32, bf16 = jnp.float32, jnp.bfloat16
@@ -399,7 +495,7 @@
     dma = pltpu.SemaphoreType.DMA
     return pl.pallas_call(
         functools.partial(kernel, nodes, heads),
-        out_shape=jax.ShapeDtypeStruct((tokens, out_weight.shape[1]), bf16),
+        out_shape=pltpu.VMEM((tokens, out_weight.shape[1]), bf16),
         in_specs=[hbm] * 6,
         out_specs=vmem,
         scratch_shapes=[
@@ -421,8 +517,10 @@
             dma((2,)),
             dma(((2 + ROWS) * COLUMNS,)),
             dma((2 + ROWS,)),
+            dma((most + 1,)),
+            dma((most, pieces)),
             dma((most,)),
-            dma((most, pieces)),
+            dma,
             dma((heads,)),
             dma((2 * ROWS * COLUMNS,)),
             dma((3,)),

time: 90.1 us -> 91.7 us (1.018); the launches traced: 89.9 us -> 90.4 us
  Pallas kernels: 88.3 us -> 89.8 us
    pallas_call x1, Pallas kernels: 88.3 us -> 89.8 us  [on_device(): pl.pallas_call(functools.partial(kernel, nodes, heads), out_shape=pltpu.V...]
where the time goes in v5:
time: 91.7 us; the launch traced here: 90.4 us
  Pallas kernels  89.8 us (98%)
    pallas_call x1, Pallas kernels, on_device(): pl.pallas_call(functools.partial(kernel, nodes, heads), out_shape=pltpu.V...  89.8 us

profile of v5, /device:TPU:33, one launch (start us, length us, event | category | flops | bytes accessed | tf_op | source)
XLA Modules:
  0.0 90.4 jit_solution(13206648681052566097)
XLA Ops:
  0.0 89.8 %attention.1 = bf16[16,2304]{1,0:T(8,128)(2,1)S(1)} custom-call(bf16[16,1152]{1,0:T(8,128)(2,1)} %query.1, bf16[16,1152]{1,0:T(8,128)(2,1)} %key.1, bf16[16,1152]{1,0:T(8,128)(2,1)} %value.1, f32[1,96]{1,0:T(1,128)} %bitcast.2, f32[1,96]{1,0:T(1,128)} %bitcast.3, bf16[576,2304]{1,0:T(8,128)(2,1)} %weight.1), custom_call_target="tpu_custom_call" | custom-call | tf_op jit(solution)/shard_map/attention/pallas_call | solution.py:496
  89.8 0.6 copy.8

commit v6 on v4

--- a/solution.py
+++ b/solution.py
@@ -13,7 +13,8 @@
 COLUMNS = 4
 ROWS = 2
 FEED_CORE = 1
-AHEAD = 5
+AHEAD = 7
+HEADS_UP = 1
 MESH = pl.DeviceIdType.MESH
 TN = (((1,), (1,)), ((), ()))
 
@@ -67,7 +68,7 @@
     group = heads * HD
     line = 2 * COLUMNS * tokens
     pieces = 2 * heads
-    steps = jnp.where(feeds_pair, nodes - 1 - AHEAD, AHEAD)
+    steps = jnp.where(feeds_pair, nodes - AHEAD, AHEAD)
 
     def device(row, column, a_core):
         return {"blk": row * COLUMNS + column, "uly": a_core}
@@ -110,6 +111,8 @@
     greets_ahead = jnp.where(feeds_pair, node != last_node, (node != 0) & (node != last_node))
     greets_behind = jnp.where(feeds_pair, node == 0, node < 2)
     lower = jnp.where(feeds_pair, node != 0, node != 1).astype(jnp.int32) + jnp.where(is_last, 1, 0)
+    over_wrap = feeds_pair & is_last
+    lower = lower + jnp.where(over_wrap, 1, 0)
 
     @pl.when(greets_ahead)
     def _():
@@ -118,6 +121,10 @@
     @pl.when(greets_behind)
     def _():
         greet(device(behind, x, core))
+
+    @pl.when(is_first & ~feeds_pair)
+    def _():
+        greet(device(behind, x, FEED_CORE))
 
     pl.semaphore_wait(barrier, ROWS * COLUMNS - jnp.where(feeds_pair, 1, 0) + lower)
 
@@ -142,7 +149,7 @@
         return pltpu.make_async_remote_copy(
             src_ref=stage.at[i, :, pl.ds(pl.multiple_of(column * lanes, PAD), window)],
             dst_ref=dst,
-            send_sem=feed_send.at[i * COLUMNS + d if i < 2 else (2 + r) * COLUMNS + d],
+            send_sem=feed_send.at[i // 2],
             recv_sem=recv,
             device_id=device(other_row(r), column, FEED_CORE),
             device_id_type=MESH,
@@ -190,36 +197,47 @@
     def _():
         sent_weight.start()
 
-    def give_back(r, d, c, h):
+    def give_back(r, d, c):
         column, a_core = other_column(d), lax.rem(core + c, 2)
         row = lax.rem(z_row + r, ROWS)
         start = row * line + (column * 2 + a_core) * tokens
         return pltpu.make_async_remote_copy(
-            src_ref=parts_out.at[h, pl.ds(pl.multiple_of(start, tokens), tokens)],
-            dst_ref=parts_in.at[core, z_row, x, h],
-            send_sem=back_send.at[h],
-            recv_sem=back_recv.at[(core * ROWS + z_row) * COLUMNS + x],
+            src_ref=parts_out.at[pl.ds(pl.multiple_of(start, tokens), tokens)],
+            dst_ref=parts_in.at[(core * ROWS + z_row) * COLUMNS + x],
+            send_sem=back_send,
+            recv_sem=back_recv,
             device_id=device(other_row(r), column, a_core),
             device_id_type=MESH,
         )
 
     backs = [(r, d, c) for r in range(ROWS) for d in range(COLUMNS) for c in range(2)]
 
-    def landing(step, p, src):
+    def landing(src, p, step, dev, send_sem):
         return pltpu.make_async_remote_copy(
-            src_ref=src,
+            src_ref=src.at[p],
             dst_ref=ring.at[step, p],
-            send_sem=ring_send.at[step],
+            send_sem=send_sem,
             recv_sem=ring_recv.at[step, p],
-            device_id=device(target, x, core),
+            device_id=dev,
             device_id_type=MESH,
         )
+
+    next_node = device(target, x, core)
+
+    def own_on(p):
+        return landing(own, p, 0, next_node, ring_send.at[0])
+
+    def own_over_wrap(p):
+        return landing(own, p, 0, device(ahead, x, 1 - core), ring_send.at[2])
+
+    def comes_last(h):
+        return feeds_pair if h >= HEADS_UP else ~feeds_pair
 
     def to_pair(ref, p):
         return pltpu.make_async_remote_copy(
             src_ref=ref,
             dst_ref=ref,
-            send_sem=pair_send.at[p],
+            send_sem=pair_send.at[p // pieces],
             recv_sem=pair_recv.at[p],
             device_id=device(z, x, 1 - core),
             device_id_type=MESH,
@@ -254,13 +272,22 @@
             return data * lax.rsqrt(meansq + 1e-06) * gain
 
         def send_own(kind):
-            for p in range(kind * heads, (kind + 1) * heads):
-
-                @pl.when(node != 0)
-                def _():
-                    landing(0, p, own.at[p]).start()
-
-                to_pair(own.at[p], p).start()
+            mine = range(kind * heads, (kind + 1) * heads)
+
+            @pl.when(is_last)
+            def _():
+                for p in mine:
+                    own_over_wrap(p).start()
+
+            @pl.when(node != 0)
+            def _():
+                for p in mine:
+                    own_on(p).start()
+
+            @pl.when(jnp.logical_not(is_last))
+            def _():
+                for p in mine:
+                    to_pair(own.at[p], p).start()
 
         pltpu.make_async_copy(key_raw, key_raw, feed_recv.at[0]).wait()
         turned[0] = key_raw[...].astype(f32).T
@@ -282,8 +309,7 @@
                 data = jnp.concatenate([data, jnp.zeros((PAD - HD, line), f32)], axis=0)
                 q_heads[h, r * line : (r + 1) * line, :] = data.T.astype(bf16)
 
-        for h in range(heads):
-            to_pair(q_heads.at[h], pieces + h).start()
+        to_pair(q_heads, pieces).start()
         sent_weight.start()
         for h in range(heads):
             attend(h, own[h], own[heads + h])
@@ -292,92 +318,111 @@
         @pl.when(node == 0)
         def _():
             for p in range(pieces):
-                landing(0, p, own.at[p]).start()
+                own_on(p).start()
 
     @pl.when(core != FEED_CORE)
     def _():
         for copy in gains:
             copy.wait()
         wait_for_target()
+
+        @pl.when(jnp.logical_not(is_last))
+        def _():
+            for p in range(pieces):
+                to_pair(own.at[p], p).wait_recv()
+                own_on(p).start()
+
+        to_pair(q_heads, pieces).wait_recv()
+
+    lane = lax.broadcasted_iota(jnp.int32, (ROWS * line, PAD), 1)
+
+    def arrives(step, p):
+        landing(own, p, step, next_node, ring_send.at[0]).wait_recv()
+
+    def chunk(step, carry):
         for p in range(pieces):
-            to_pair(own.at[p], p).wait_recv()
-            landing(0, p, own.at[p]).start()
-        for h in range(heads):
-            to_pair(q_heads.at[h], pieces + h).wait_recv()
-
-    lane = lax.broadcasted_iota(jnp.int32, (ROWS * line, PAD), 1)
-
-    def ring_step(step, last):
-        for p in range(pieces):
-            landing(step, p, own.at[p]).wait_recv()
-            if not last:
-                landing(step + 1, p, ring.at[step, p]).start()
+            arrives(step, p)
+
+            @pl.when(step < steps - 2)
+            def _():
+                landing(ring.at[step], p, step + 1, next_node, ring_send.at[0]).start()
+
+            @pl.when((step == steps - 2) & comes_last(p % heads))
+            def _():
+                landing(ring.at[step], p, step + 1, next_node, ring_send.at[1]).start()
+
             if p >= heads:
-                h = p - heads
-                attend(h, ring[step, h], ring[step, p])
-                if last:
-                    total = totals[h]
-                    high = total.astype(bf16)
-                    low = (total - high.astype(f32)).astype(bf16)
-                    parts_out[h] = jnp.where(lane >= HD + 16, low, high)
-                    for r, d, c in backs:
-                        if (r, d, c) != (0, 0, 0):
-                            give_back(r, d, c, h).start()
-
-    def chunk(step, carry):
-        ring_step(step, False)
+                attend(p - heads, ring[step, p - heads], ring[step, p])
         return carry
 
     lax.fori_loop(0, steps - 1, chunk, 0)
-    ring_step(steps - 1, True)
+    for h in range(heads):
+
+        @pl.when(comes_last(h))
+        def _():
+            arrives(steps - 1, h)
+            arrives(steps - 1, heads + h)
+            attend(h, ring[steps - 1, h], ring[steps - 1, heads + h])
+
+        total = totals[h]
+        high = total.astype(bf16)
+        low = (total - high.astype(f32)).astype(bf16)
+        parts_out[:, h * PAD : (h + 1) * PAD] = jnp.where(lane >= HD + 16, low, high)
+
+    for r, d, c in backs:
+        if (r, d, c) != (0, 0, 0):
+            give_back(r, d, c).start()
     own_start = z_row * line + (x * 2 + core) * tokens
-    for h in range(heads):
-        parts_in[core, z_row, x, h] = parts_out[h, pl.ds(pl.multiple_of(own_start, tokens), tokens)]
-
-    for i, r, d in feeds:
-        if (r, d) == (0, 0):
-
-            @pl.when(core != FEED_CORE)
-            def _():
-                feed(i, r, d).wait_send()
-
-        else:
-            feed(i, r, d).wait_send()
+    parts_in[(core * ROWS + z_row) * COLUMNS + x] = parts_out[
+        pl.ds(pl.multiple_of(own_start, tokens), tokens)
+    ]
+
+    def left(ref, sem):
+        pltpu.make_async_copy(ref, ref, sem).wait()
 
     @pl.when(feeds_pair)
     def _():
-        for p in range(pieces):
-            to_pair(own.at[p], p).wait_send()
-        for h in range(heads):
-            to_pair(q_heads.at[h], pieces + h).wait_send()
-
-    def sent(step, carry):
-        pltpu.make_async_copy(ring.at[step], ring.at[step], ring_send.at[step]).wait()
-        return carry
-
-    lax.fori_loop(0, steps, sent, 0)
-    for h in range(heads):
-        others = parts_out.at[h, 0 : (len(backs) - 1) * tokens]
-        pltpu.make_async_copy(others, others, back_send.at[h]).wait()
+        ways = COLUMNS - 1
+        left(key_raw.at[0 : 2 * ways * tokens], feed_send.at[0])
+        left(key_raw.at[0 : (ROWS * COLUMNS - 1) * tokens], feed_send.at[1])
+        left(q_heads, pair_send.at[1])
+        left(ring.at[0 : nodes - AHEAD - 1], ring_send.at[0])
+        left(ring.at[0, 0 : 2 * (heads - HEADS_UP)], ring_send.at[1])
+
+        @pl.when(is_last)
+        def _():
+            left(own, ring_send.at[2])
+
+        @pl.when(jnp.logical_not(is_last))
+        def _():
+            left(own, pair_send.at[0])
+
+    @pl.when(core != FEED_CORE)
+    def _():
+        left(key_raw.at[0 : 2 * COLUMNS * tokens], feed_send.at[0])
+        left(key_raw.at[0 : ROWS * COLUMNS * tokens], feed_send.at[1])
+        left(ring.at[0, 0 : 2 * HEADS_UP], ring_send.at[1])
+
+        @pl.when(is_last)
+        def _():
+            left(ring.at[0 : AHEAD - 2], ring_send.at[0])
+
+        @pl.when(jnp.logical_not(is_last))
+        def _():
+            left(ring.at[0 : AHEAD - 1], ring_send.at[0])
+
+    left(parts_out.at[0 : (len(backs) - 1) * tokens], back_send)
 
     local_weight.wait()
     sent_weight.wait()
     attn = []
-    sources = [(c, r, d) for c in range(2) for r in range(ROWS) for d in range(COLUMNS)]
-    for i, (c, r, d) in enumerate(sources):
-        itself = (z_row == r) & (x == d) & (core == c)
-
-        @pl.when(jnp.logical_not(itself))
-        def _():
-            part = parts_in.at[c, r, d]
-            pltpu.make_async_copy(part, part, back_recv.at[i]).wait()
-
+    others = parts_in.at[0 : len(backs) - 1]
+    pltpu.make_async_copy(others, others, back_recv).wait()
     for d in range(COLUMNS):
         for h in range(heads):
             part = sum(
-                parts_in[c, r, d, h].astype(f32)
-                for c in range(2)
-                for r in range(ROWS)
+                parts_in[i * COLUMNS + d, :, h * PAD : (h + 1) * PAD].astype(f32)
+                for i in range(2 * ROWS)
             )
             total_weight = part[:, HD : HD + 1] + part[:, HD + 16 : HD + 17]
             attn.append((part[:, 0:HD] / total_weight).astype(bf16))
@@ -390,7 +435,7 @@
     heads = width // HD // COLUMNS
     nodes = lines // ROWS
     pieces = 2 * heads
-    most = max(AHEAD, nodes - 1 - AHEAD)
+    most = max(AHEAD, nodes - AHEAD)
     line = 2 * COLUMNS * tokens
     window = 3 * PAD
     f32, bf16 = jnp.float32, jnp.bfloat16
@@ -399,7 +444,7 @@
     dma = pltpu.SemaphoreType.DMA
     return pl.pallas_call(
         functools.partial(kernel, nodes, heads),
-        out_shape=jax.ShapeDtypeStruct((tokens, out_weight.shape[1]), bf16),
+        out_shape=pltpu.VMEM((tokens, out_weight.shape[1]), bf16),
         in_specs=[hbm] * 6,
         out_specs=vmem,
         scratch_shapes=[
@@ -414,20 +459,20 @@
             pltpu.VMEM((most, pieces, HD, line), bf16),
             pltpu.VMEM((heads, ROWS * line, PAD), bf16),
             pltpu.VMEM((heads, ROWS * line, PAD), f32),
-            pltpu.VMEM((heads, ROWS * line, PAD), bf16),
-            pltpu.VMEM((2, ROWS, COLUMNS, heads, tokens, PAD), bf16),
+            pltpu.VMEM((ROWS * line, heads * PAD), bf16),
+            pltpu.VMEM((2 * ROWS * COLUMNS, tokens, heads * PAD), bf16),
             pltpu.VMEM((2 * out_weight.shape[0], out_weight.shape[1]), bf16),
             dma((3,)),
             dma((2,)),
-            dma(((2 + ROWS) * COLUMNS,)),
+            dma((2,)),
             dma((2 + ROWS,)),
-            dma((most,)),
+            dma((3,)),
             dma((most, pieces)),
-            dma((heads,)),
-            dma((2 * ROWS * COLUMNS,)),
+            dma,
+            dma,
             dma((3,)),
-            dma((pieces + heads,)),
-            dma((pieces + heads,)),
+            dma((2,)),
+            dma((pieces + 1,)),
             pltpu.SemaphoreType.REGULAR,
         ],
         compiler_params=pltpu.CompilerParams(collective_id=0, has_side_effects=True),

time: 90.1 us -> 84.8 us (0.941)
  Pallas kernels: 88.3 us -> 83.9 us
    pallas_call x1, Pallas kernels: 88.3 us -> 83.9 us  [on_device(): pl.pallas_call(functools.partial(kernel, nodes, heads), out_shape=pltpu.V...]
where the time goes in v6:
time: 84.8 us; the launch traced here: 84.6 us
  Pallas kernels  83.9 us (99%)
    pallas_call x1, Pallas kernels, on_device(): pl.pallas_call(functools.partial(kernel, nodes, heads), out_shape=pltpu.V...  83.9 us

profile of v6, /device:TPU:33, one launch (start us, length us, event | category | flops | bytes accessed | tf_op | source)
XLA Modules:
  0.0 84.6 jit_solution(5686561039214670133)
XLA Ops:
  0.0 83.9 %attention.1 = bf16[16,2304]{1,0:T(8,128)(2,1)S(1)} custom-call(bf16[16,1152]{1,0:T(8,128)(2,1)} %query.1, bf16[16,1152]{1,0:T(8,128)(2,1)} %key.1, bf16[16,1152]{1,0:T(8,128)(2,1)} %value.1, f32[1,96]{1,0:T(1,128)} %bitcast.2, f32[1,96]{1,0:T(1,128)} %bitcast.3, bf16[576,2304]{1,0:T(8,128)(2,1)} %weight.1), custom_call_target="tpu_custom_call" | custom-call | tf_op jit(solution)/shard_map/attention/pallas_call | solution.py:445
  83.9 0.6 copy.8

commit v7 on v6

--- a/solution.py
+++ b/solution.py
@@ -197,13 +197,13 @@
     def _():
         sent_weight.start()
 
-    def give_back(r, d, c):
+    def give_back(r, d, c, h):
         column, a_core = other_column(d), lax.rem(core + c, 2)
         row = lax.rem(z_row + r, ROWS)
         start = row * line + (column * 2 + a_core) * tokens
         return pltpu.make_async_remote_copy(
-            src_ref=parts_out.at[pl.ds(pl.multiple_of(start, tokens), tokens)],
-            dst_ref=parts_in.at[(core * ROWS + z_row) * COLUMNS + x],
+            src_ref=parts_out.at[h, pl.ds(pl.multiple_of(start, tokens), tokens)],
+            dst_ref=parts_in.at[(core * ROWS + z_row) * COLUMNS + x, h],
             send_sem=back_send,
             recv_sem=back_recv,
             device_id=device(other_row(r), column, a_core),
@@ -279,7 +279,7 @@
                 for p in mine:
                     own_over_wrap(p).start()
 
-            @pl.when(node != 0)
+            @pl.when((node != 0) & (z_row != 1))
             def _():
                 for p in mine:
                     own_on(p).start()
@@ -309,6 +309,12 @@
                 data = jnp.concatenate([data, jnp.zeros((PAD - HD, line), f32)], axis=0)
                 q_heads[h, r * line : (r + 1) * line, :] = data.T.astype(bf16)
 
+
+        @pl.when((node != 0) & (z_row == 1))
+        def _():
+            for p in range(pieces):
+                own_on(p).start()
+
         to_pair(q_heads, pieces).start()
         sent_weight.start()
         for h in range(heads):
@@ -356,6 +362,22 @@
         return carry
 
     lax.fori_loop(0, steps - 1, chunk, 0)
+
+    def give(h):
+        total = totals[h]
+        high = total.astype(bf16)
+        low = (total - high.astype(f32)).astype(bf16)
+        parts_out[h] = jnp.where(lane >= HD + 16, low, high)
+        for r, d, c in backs:
+            if (r, d, c) != (0, 0, 0):
+                give_back(r, d, c, h).start()
+
+    for h in range(heads):
+
+        @pl.when(jnp.logical_not(comes_last(h)))
+        def _():
+            give(h)
+
     for h in range(heads):
 
         @pl.when(comes_last(h))
@@ -363,19 +385,13 @@
             arrives(steps - 1, h)
             arrives(steps - 1, heads + h)
             attend(h, ring[steps - 1, h], ring[steps - 1, heads + h])
-
-        total = totals[h]
-        high = total.astype(bf16)
-        low = (total - high.astype(f32)).astype(bf16)
-        parts_out[:, h * PAD : (h + 1) * PAD] = jnp.where(lane >= HD + 16, low, high)
-
-    for r, d, c in backs:
-        if (r, d, c) != (0, 0, 0):
-            give_back(r, d, c).start()
+            give(h)
+
     own_start = z_row * line + (x * 2 + core) * tokens
-    parts_in[(core * ROWS + z_row) * COLUMNS + x] = parts_out[
-        pl.ds(pl.multiple_of(own_start, tokens), tokens)
-    ]
+    for h in range(heads):
+        parts_in[(core * ROWS + z_row) * COLUMNS + x, h] = parts_out[
+            h, pl.ds(pl.multiple_of(own_start, tokens), tokens)
+        ]
 
     def left(ref, sem):
         pltpu.make_async_copy(ref, ref, sem).wait()
@@ -411,7 +427,7 @@
         def _():
             left(ring.at[0 : AHEAD - 1], ring_send.at[0])
 
-    left(parts_out.at[0 : (len(backs) - 1) * tokens], back_send)
+    left(parts_out.at[:, 0 : (len(backs) - 1) * tokens], back_send)
 
     local_weight.wait()
     sent_weight.wait()
@@ -421,7 +437,7 @@
     for d in range(COLUMNS):
         for h in range(heads):
             part = sum(
-                parts_in[i * COLUMNS + d, :, h * PAD : (h + 1) * PAD].astype(f32)
+                parts_in[i * COLUMNS + d, h].astype(f32)
                 for i in range(2 * ROWS)
             )
             total_weight = part[:, HD : HD + 1] + part[:, HD + 16 : HD + 17]
@@ -459,8 +475,8 @@
             pltpu.VMEM((most, pieces, HD, line), bf16),
             pltpu.VMEM((heads, ROWS * line, PAD), bf16),
             pltpu.VMEM((heads, ROWS * line, PAD), f32),
-            pltpu.VMEM((ROWS * line, heads * PAD), bf16),
-            pltpu.VMEM((2 * ROWS * COLUMNS, tokens, heads * PAD), bf16),
+            pltpu.VMEM((heads, ROWS * line, PAD), bf16),
+            pltpu.VMEM((2 * ROWS * COLUMNS, heads, tokens, PAD), bf16),
             pltpu.VMEM((2 * out_weight.shape[0], out_weight.shape[1]), bf16),
             dma((3,)),
             dma((2,)),

time: 84.8 us -> 82 us (0.967)
  Pallas kernels: 83.9 us -> 81.2 us
    pallas_call x1, Pallas kernels: 83.9 us -> 81.2 us  [on_device(): pl.pallas_call(functools.partial(kernel, nodes, heads), out_shape=pltpu.V...]
where the time goes in v7:
time: 82 us; the launch traced here: 81.8 us
  Pallas kernels  81.2 us (99%)
    pallas_call x1, Pallas kernels, on_device(): pl.pallas_call(functools.partial(kernel, nodes, heads), out_shape=pltpu.V...  81.2 us

profile of v7, /device:TPU:33, one launch (start us, length us, event | category | flops | bytes accessed | tf_op | source)
XLA Modules:
  0.0 81.8 jit_solution(12701545079752107693)
XLA Ops:
  0.0 81.2 %attention.1 = bf16[16,2304]{1,0:T(8,128)(2,1)S(1)} custom-call(bf16[16,1152]{1,0:T(8,128)(2,1)} %query.1, bf16[16,1152]{1,0:T(8,128)(2,1)} %key.1, bf16[16,1152]{1,0:T(8,128)(2,1)} %value.1, f32[1,96]{1,0:T(1,128)} %bitcast.2, f32[1,96]{1,0:T(1,128)} %bitcast.3, bf16[576,2304]{1,0:T(8,128)(2,1)} %weight.1), custom_call_target="tpu_custom_call" | custom-call | tf_op jit(solution)/shard_map/attention/pallas_call | solution.py:461
  81.2 0.6 copy.8

commit v8 on v7

--- a/solution.py
+++ b/solution.py
@@ -13,8 +13,8 @@
 COLUMNS = 4
 ROWS = 2
 FEED_CORE = 1
-AHEAD = 7
-HEADS_UP = 1
+AHEAD = 6
+HEADS_UP = 3
 MESH = pl.DeviceIdType.MESH
 TN = (((1,), (1,)), ((), ()))
 
@@ -55,6 +55,7 @@
     pair_send,
     pair_recv,
     ready,
+    row_ready,
 ):
     f32, bf16 = jnp.float32, jnp.bfloat16
     block = lax.axis_index("blk")
@@ -68,7 +69,8 @@
     group = heads * HD
     line = 2 * COLUMNS * tokens
     pieces = 2 * heads
-    steps = jnp.where(feeds_pair, nodes - AHEAD, AHEAD)
+    split = HEADS_UP < heads
+    steps = jnp.where(feeds_pair, nodes - AHEAD - (0 if split else 1), AHEAD)
 
     def device(row, column, a_core):
         return {"blk": row * COLUMNS + column, "uly": a_core}
@@ -100,13 +102,30 @@
     def greet(dev):
         pl.semaphore_signal(barrier, inc=1, device_id=dev, device_id_type=MESH)
 
+    first_row = z_row == 0
+
     @pl.when(feeds_pair)
     def _():
-        for r in range(ROWS):
-            for d in range(COLUMNS):
-                for c in range(2):
-                    if (r, d, c) != (0, 0, 0):
-                        greet(device(other_row(r), other_column(d), lax.rem(core + c, 2)))
+        for d in range(COLUMNS):
+            for c in range(2):
+                if (d, c) != (0, 0):
+                    greet(device(z, other_column(d), lax.rem(core + c, 2)))
+
+    @pl.when(first_row & (feeds_pair | (node != 0)))
+    def _():
+        for d in range(COLUMNS):
+            greet(device(z + 1, other_column(d), FEED_CORE))
+
+    @pl.when(first_row & feeds_pair)
+    def _():
+        for d in range(COLUMNS):
+            greet(device(z + 1, other_column(d), 1 - FEED_CORE))
+
+    before = jnp.where(
+        feeds_pair,
+        jnp.where(first_row, COLUMNS - 1, jnp.where(is_first, 2, 3) * COLUMNS - 1),
+        jnp.where(first_row, COLUMNS, 2 * COLUMNS),
+    )
 
     greets_ahead = jnp.where(feeds_pair, node != last_node, (node != 0) & (node != last_node))
     greets_behind = jnp.where(feeds_pair, node == 0, node < 2)
@@ -126,7 +145,19 @@
     def _():
         greet(device(behind, x, FEED_CORE))
 
-    pl.semaphore_wait(barrier, ROWS * COLUMNS - jnp.where(feeds_pair, 1, 0) + lower)
+    pl.semaphore_wait(barrier, before + lower)
+
+    def tell(row, column, a_core, times):
+        pl.semaphore_signal(
+            row_ready, inc=times, device_id=device(row, column, a_core), device_id_type=MESH
+        )
+
+    for c in range(2):
+
+        @pl.when(feeds_pair & ~first_row & ((node != 0) | (c == FEED_CORE)))
+        def _():
+            for d in range(COLUMNS):
+                tell(z - 1, other_column(d), c, 1)
 
     target = jnp.where(feeds_pair, behind, ahead)
     source = jnp.where(feeds_pair, ahead, behind)
@@ -167,6 +198,12 @@
     for i, r, d in feeds:
         if (r, d) == (0, 2):
             staged[i].wait()
+        if (r, d) == (1, 2):
+
+            @pl.when(first_row)
+            def _():
+                pl.semaphore_wait(row_ready, COLUMNS)
+
         if (r, d) == (0, 0):
 
             @pl.when(feeds_pair)
@@ -231,7 +268,7 @@
         return landing(own, p, 0, device(ahead, x, 1 - core), ring_send.at[2])
 
     def comes_last(h):
-        return feeds_pair if h >= HEADS_UP else ~feeds_pair
+        return feeds_pair | ~feeds_pair if not split else feeds_pair if h >= HEADS_UP else ~feeds_pair
 
     def to_pair(ref, p):
         return pltpu.make_async_remote_copy(
@@ -279,17 +316,29 @@
                 for p in mine:
                     own_over_wrap(p).start()
 
-            @pl.when((node != 0) & (z_row != 1))
+            @pl.when((node != 0) & first_row)
             def _():
                 for p in mine:
                     own_on(p).start()
 
+            if kind == 1:
+
+                @pl.when((node != 0) & ~first_row)
+                def _():
+                    for p in range(pieces):
+                        own_on(p).start()
+
             @pl.when(jnp.logical_not(is_last))
             def _():
                 for p in mine:
                     to_pair(own.at[p], p).start()
 
         pltpu.make_async_copy(key_raw, key_raw, feed_recv.at[0]).wait()
+
+        @pl.when(is_first & first_row)
+        def _():
+            tell(z, x, 1 - FEED_CORE, COLUMNS)
+
         turned[0] = key_raw[...].astype(f32).T
         for h in range(heads):
             own[h] = normed(head_of(0, h), k_column).astype(bf16)
@@ -309,12 +358,6 @@
                 data = jnp.concatenate([data, jnp.zeros((PAD - HD, line), f32)], axis=0)
                 q_heads[h, r * line : (r + 1) * line, :] = data.T.astype(bf16)
 
-
-        @pl.when((node != 0) & (z_row == 1))
-        def _():
-            for p in range(pieces):
-                own_on(p).start()
-
         to_pair(q_heads, pieces).start()
         sent_weight.start()
         for h in range(heads):
@@ -402,8 +445,8 @@
         left(key_raw.at[0 : 2 * ways * tokens], feed_send.at[0])
         left(key_raw.at[0 : (ROWS * COLUMNS - 1) * tokens], feed_send.at[1])
         left(q_heads, pair_send.at[1])
-        left(ring.at[0 : nodes - AHEAD - 1], ring_send.at[0])
-        left(ring.at[0, 0 : 2 * (heads - HEADS_UP)], ring_send.at[1])
+        left(ring.at[0 : nodes - AHEAD - (1 if split else 2)], ring_send.at[0])
+        left(ring.at[0, 0 : 2 * (heads - HEADS_UP) if split else pieces], ring_send.at[1])
 
         @pl.when(is_last)
         def _():
@@ -490,6 +533,7 @@
             dma((2,)),
             dma((pieces + 1,)),
             pltpu.SemaphoreType.REGULAR,
+            pltpu.SemaphoreType.REGULAR,
         ],
         compiler_params=pltpu.CompilerParams(collective_id=0, has_side_effects=True),
         name="attention",

time: 82 us -> 81 us (0.988)
  Pallas kernels: 81.2 us -> 80.2 us
    pallas_call x1, Pallas kernels: 81.2 us -> 80.2 us  [on_device(): pl.pallas_call(functools.partial(kernel, nodes, heads), out_shape=pltpu.V...]
where the time goes in v8:
time: 81 us; the launch traced here: 80.8 us
  Pallas kernels  80.2 us (99%)
    pallas_call x1, Pallas kernels, on_device(): pl.pallas_call(functools.partial(kernel, nodes, heads), out_shape=pltpu.V...  80.2 us

profile of v8, /device:TPU:33, one launch (start us, length us, event | category | flops | bytes accessed | tf_op | source)
XLA Modules:
  0.0 80.8 jit_solution(12499129332151059919)
XLA Ops:
  0.0 80.2 %attention.1 = bf16[16,2304]{1,0:T(8,128)(2,1)S(1)} custom-call(bf16[16,1152]{1,0:T(8,128)(2,1)} %query.1, bf16[16,1152]{1,0:T(8,128)(2,1)} %key.1, bf16[16,1152]{1,0:T(8,128)(2,1)} %value.1, f32[1,96]{1,0:T(1,128)} %bitcast.2, f32[1,96]{1,0:T(1,128)} %bitcast.3, bf16[576,2304]{1,0:T(8,128)(2,1)} %weight.1), custom_call_target="tpu_custom_call" | custom-call | tf_op jit(solution)/shard_map/attention/pallas_call | solution.py:504
  80.2 0.6 copy.8

commit v9 on v8

--- a/solution.py
+++ b/solution.py
@@ -247,7 +247,7 @@
             device_id_type=MESH,
         )
 
-    backs = [(r, d, c) for r in range(ROWS) for d in range(COLUMNS) for c in range(2)]
+    backs = [(r, d, c) for r in (1, 0) for d in (2, 1, 3, 0) for c in range(2)]
 
     def landing(src, p, step, dev, send_sem):
         return pltpu.make_async_remote_copy(
@@ -494,7 +494,7 @@
     heads = width // HD // COLUMNS
     nodes = lines // ROWS
     pieces = 2 * heads
-    most = max(AHEAD, nodes - AHEAD)
+    most = max(AHEAD, nodes - AHEAD - (0 if HEADS_UP < heads else 1))
     line = 2 * COLUMNS * tokens
     window = 3 * PAD
     f32, bf16 = jnp.float32, jnp.bfloat16

time: 81 us -> 80.7 us (level)
  no operation moved by 1% of the time
where the time goes in v9:
time: 80.7 us; the launch traced here: 80.5 us
  Pallas kernels  79.8 us (99%)
    pallas_call x1, Pallas kernels, on_device(): pl.pallas_call(functools.partial(kernel, nodes, heads), out_shape=pltpu.V...  79.8 us

profile of v9, /device:TPU:33, one launch (start us, length us, event | category | flops | bytes accessed | tf_op | source)
XLA Modules:
  0.0 80.5 jit_solution(11814619125908662568)
XLA Ops:
  0.0 79.8 %attention.1 = bf16[16,2304]{1,0:T(8,128)(2,1)S(1)} custom-call(bf16[16,1152]{1,0:T(8,128)(2,1)} %query.1, bf16[16,1152]{1,0:T(8,128)(2,1)} %key.1, bf16[16,1152]{1,0:T(8,128)(2,1)} %value.1, f32[1,96]{1,0:T(1,128)} %bitcast.2, f32[1,96]{1,0:T(1,128)} %bitcast.3, bf16[576,2304]{1,0:T(8,128)(2,1)} %weight.1), custom_call_target="tpu_custom_call" | custom-call | tf_op jit(solution)/shard_map/attention/pallas_call | solution.py:504
  79.8 0.6 copy.8

commit v10 on v9

--- a/solution.py
+++ b/solution.py
@@ -316,17 +316,10 @@
                 for p in mine:
                     own_over_wrap(p).start()
 
-            @pl.when((node != 0) & first_row)
+            @pl.when(node != 0)
             def _():
                 for p in mine:
                     own_on(p).start()
-
-            if kind == 1:
-
-                @pl.when((node != 0) & ~first_row)
-                def _():
-                    for p in range(pieces):
-                        own_on(p).start()
 
             @pl.when(jnp.logical_not(is_last))
             def _():

time: 80.7 us -> 80.7 us (level)
  no operation moved by 1% of the time
where the time goes in v10:
time: 80.7 us; the launch traced here: 80.6 us
  Pallas kernels  79.9 us (99%)
    pallas_call x1, Pallas kernels, on_device(): pl.pallas_call(functools.partial(kernel, nodes, heads), out_shape=pltpu.V...  79.9 us

profile of v10, /device:TPU:33, one launch (start us, length us, event | category | flops | bytes accessed | tf_op | source)
XLA Modules:
  0.0 80.6 jit_solution(16553869038573048265)
XLA Ops:
  0.0 79.9 %attention.1 = bf16[16,2304]{1,0:T(8,128)(2,1)S(1)} custom-call(bf16[16,1152]{1,0:T(8,128)(2,1)} %query.1, bf16[16,1152]{1,0:T(8,128)(2,1)} %key.1, bf16[16,1152]{1,0:T(8,128)(2,1)} %value.1, f32[1,96]{1,0:T(1,128)} %bitcast.2, f32[1,96]{1,0:T(1,128)} %bitcast.3, bf16[576,2304]{1,0:T(8,128)(2,1)} %weight.1), custom_call_target="tpu_custom_call" | custom-call | tf_op jit(solution)/shard_map/attention/pallas_call | solution.py:497
  79.9 0.6 copy.8
